TPU v7x, 32 devices: a whole 2x2x4 slice. The times are simulated.
32 devices in a mesh: energy: 8 (over y, x, core), cell: 4 (over z).
Axes of the slice: x: 2, y: 2, z: 4, core: 2. Of those that a mesh axis runs over, the one named last changes fastest.
Arguments:
- g_retarded: bfloat16 [2, 8, 4, 128, 512], P(None, 'energy', None, None, 'cell'), may hold values from -0.75 to 0.75
- sigma_lesser: bfloat16 [2, 8, 128, 512], P(None, 'energy', None, 'cell'), may hold values from -1.5 to 1.5
- w_screened: bfloat16 [2, 8, 4, 128, 512], P(None, 'energy', None, None, 'cell'), may hold values from -0.75 to 0.75
- coupling: int32 [4, 4], replicated, may hold values 0 or 1
Outputs:
- polarization: bfloat16 [4, 2, 8, 16384], P('cell', None, 'energy')
- w_lesser: bfloat16 [4, 2, 8, 128, 128], P('cell', None, 'energy')
Inputs may be any that keep to these rules, and one draw needn't show every extreme that they name: coupling[i, j] is 1 where cell i is coupled to cell j and 0 elsewhere.
All inputs are finite; a program needn't handle non-finite values.
Results may differ from a plain program's by a relative error of at most 0.024.
Values may be sent and summed in bfloat16 or wider, within the bound.
No kernel may reach another device: no remote copies, remote signals or barrier semaphores. Data moves between devices by JAX's collectives and lax.ppermute only.
A program may use at most 64 MiB of HBM per device.

v0:
```python
import math

import jax
import jax.numpy as jnp
from jax import lax
from jax.sharding import PartitionSpec as P


def forward_product(left, right):
    return jnp.einsum("eibjc,ecjd->eibjd", left, right, preferred_element_type=jnp.float32)


def adjoint_product(left, right):
    return jnp.einsum("eibjc,eidjc->iebd", left, right, preferred_element_type=jnp.float32)


def sandwich_rows(columns, sources, coupling, cell_index, count):
    orbitals = sources.shape[2]
    local_cells = sources.shape[3] // orbitals
    energies = sources.shape[1]
    rows_block = columns
    rows_block = rows_block.reshape(2, energies, count, orbitals, local_cells, orbitals)
    col_re = rows_block[0]
    col_im = rows_block[1]
    source = sources.reshape(2, energies, orbitals, local_cells, orbitals)
    src_re = source[0]
    src_im = source[1]
    mid_re = (forward_product(col_re, src_re) - forward_product(col_im, src_im)).astype(
        jnp.bfloat16
    )
    mid_im = (forward_product(col_re, src_im) + forward_product(col_im, src_re)).astype(
        jnp.bfloat16
    )
    weight = lax.dynamic_slice(coupling, (0, cell_index * local_cells), (count, local_cells))
    weight = weight.astype(jnp.bfloat16)[None, :, None, :, None]
    mid_re = mid_re * weight
    mid_im = mid_im * weight
    part_re = adjoint_product(mid_re, col_re) + adjoint_product(mid_im, col_im)
    part_im = adjoint_product(mid_im, col_re) - adjoint_product(mid_re, col_im)
    return jnp.stack([part_re, part_im], axis=1)


def correlate_spectral(spread):
    energies = spread.shape[2]
    length = 2 * energies
    freqs = jnp.arange(length, dtype=jnp.int32)[:, None]
    points = jnp.arange(energies, dtype=jnp.int32)[None, :]
    phase = jnp.mod(freqs * points, length).astype(jnp.float32) * (math.pi / energies)
    cos_table = jnp.cos(phase)
    sin_table = jnp.sin(phase)
    cos_high = cos_table.astype(jnp.bfloat16)
    cos_low = (cos_table - cos_high.astype(jnp.float32)).astype(jnp.bfloat16)
    sin_high = sin_table.astype(jnp.bfloat16)
    sin_low = (sin_table - sin_high.astype(jnp.float32)).astype(jnp.bfloat16)

    def forward(high, low, data):
        upper = jnp.einsum("ft,ctk->cfk", high, data, preferred_element_type=jnp.float32)
        return upper + jnp.einsum("ft,ctk->cfk", low, data, preferred_element_type=jnp.float32)

    def inverse(table, data):
        return jnp.einsum("ft,cfk->ctk", table, data, precision=lax.Precision.HIGH)

    low_re = spread[:, 0]
    low_im = spread[:, 1]
    high_re = spread[:, 2]
    high_im = spread[:, 3]
    spec_a_re = forward(cos_high, cos_low, low_re) + forward(sin_high, sin_low, low_im)
    spec_a_im = forward(cos_high, cos_low, low_im) - forward(sin_high, sin_low, low_re)
    spec_b_re = forward(cos_high, cos_low, high_re) + forward(sin_high, sin_low, high_im)
    spec_b_im = forward(cos_high, cos_low, high_im) - forward(sin_high, sin_low, high_re)
    cross_re = spec_a_re * spec_b_re + spec_a_im * spec_b_im
    cross_im = spec_a_im * spec_b_re - spec_a_re * spec_b_im
    back_re = (inverse(cos_table, cross_re) - inverse(sin_table, cross_im)) / length
    back_im = (inverse(cos_table, cross_im) + inverse(sin_table, cross_re)) / length
    factor = 1.0 / math.sqrt(energies)
    return jnp.stack([back_im * factor, -back_re * factor], axis=1)


def on_device(g_retarded, sigma_lesser, w_screened, coupling):
    cell_index = lax.axis_index("cell")
    orbitals = sigma_lesser.shape[2]
    local_cells = sigma_lesser.shape[3] // orbitals
    energies_dev = sigma_lesser.shape[1]
    lesser = lax.psum_scatter(
        sandwich_rows(
            g_retarded, sigma_lesser, coupling, cell_index, local_cells * lax.axis_size("cell")
        ).astype(jnp.bfloat16),
        "cell",
        scatter_dimension=0,
        tiled=True,
    ).astype(jnp.float32)
    row_block = lax.dynamic_slice_in_dim(g_retarded, cell_index * local_cells + 0, 1, 2)
    blocks = [row_block[:, :, 0, :, 0:orbitals]]
    diagonal = jnp.stack(blocks, axis=0).astype(jnp.float32)
    diag_re = diagonal[:, 0]
    diag_im = diagonal[:, 1]
    greater = lesser + jnp.stack(
        [diag_re - jnp.swapaxes(diag_re, -1, -2), diag_im + jnp.swapaxes(diag_im, -1, -2)], axis=1
    )
    both = jnp.concatenate([lesser, greater], axis=1).astype(jnp.bfloat16)
    flat = both.reshape(local_cells, 4, energies_dev, orbitals * orbitals)
    spread = lax.all_to_all(flat, "energy", split_axis=3, concat_axis=2, tiled=True)
    polar = correlate_spectral(spread).astype(jnp.bfloat16)
    polar_local = lax.all_to_all(polar, "energy", split_axis=2, concat_axis=3, tiled=True)
    sources = polar_local.reshape(local_cells, 2, energies_dev, orbitals, orbitals)
    sources = jnp.transpose(sources, (1, 2, 3, 0, 4)).reshape(
        2, energies_dev, orbitals, local_cells * orbitals
    )
    screened = lax.psum_scatter(
        sandwich_rows(
            w_screened, sources, coupling, cell_index, local_cells * lax.axis_size("cell")
        ).astype(jnp.bfloat16),
        "cell",
        scatter_dimension=0,
        tiled=True,
    )
    return (polar_local, screened)


def solution(mesh):
    return jax.shard_map(
        on_device,
        mesh=mesh,
        in_specs=(
            P(None, "energy", None, None, "cell"),
            P(None, "energy", None, "cell"),
            P(None, "energy", None, None, "cell"),
            P(),
        ),
        out_specs=(P("cell", None, "energy", None), P("cell", None, "energy", None, None)),
        check_vma=False,
    )
```

profile of v0, /device:TPU:0, one launch (start us, length us, event | category | flops | bytes accessed | tf_op | source)
XLA Modules:
  0.0 264.8 jit_solution(17689031934140179815)
XLA Ops:
  7.2 1.1 fusion.61
  8.3 1.1 fusion.65
  9.5 0.9 fusion.127
  10.4 1.1 fusion.31
  11.5 1.1 fusion.59
  12.6 1.1 fusion.29
  13.8 1.1 fusion.63
  14.9 1.1 fusion.24
  16.1 1.1 fusion.25
  17.2 0.7 pad_maximum_fusion
  18.0 0.9 constant_dynamic-slice_fusion.1
  19.4 1.2 dynamic-slice
  20.6 35.8 %all-reduce.5.cloned.1.call-done = bf16[4,2,1,128,128]{4,3,0,2,1:T(8,128)(2,1)} async-done(((bf16[4,2,1,128,128]{4,3,0,2,1:T(8,128)(2,1)}), bf16[4,2,1,128,128]{4,3,0,2,1:T(8,128)(2,1)}) %all-reduce.5.cloned.1.call-update) | async-done | bytes 262160
  56.4 1.5 fusion.36
  58.2 12.9 %copy.76 = bf16[1,4,1,16384]{1,2,0,3:T(2,128)(2,1)} copy(bf16[1,4,1,16384]{3,1,2,0:T(4,128)(2,1)S(1)} %pad_maximum_fusion.2) | data formatting | bytes 262144 | tf_op jit(solution)/shard_map/concatenate | solution.py:100
  71.0 0.5 broadcast.79
  71.6 90.8 %reduce.6 = bf16[16384,4]{1,0:T(8,128)(2,1)} reduce(bf16[16384,1,1,4]{3,2,1,0:T(2,128)(2,1)} %bitcast.233, bf16[]{:T(256)} %broadcast.79), dimensions={1,2}, to_apply=%bitcast.220.reduce_sub_computation | reduce | bytes 262146
  162.3 8.7 %reshape.445 = bf16[8,2,4096]{2,1,0:T(2,128)(2,1)S(1)} reshape(bf16[16384,4]{1,0:T(8,128)(2,1)} %reduce.6) | data formatting | bytes 262144
  171.0 9.0 %all_to_all.24 = bf16[8,2,4096]{2,1,0:T(2,128)(2,1)S(1)} all-to-all(bf16[8,2,4096]{2,1,0:T(2,128)(2,1)S(1)} %reshape.445), channel_id=1, replica_groups=mesh['energy'=8,'cell'=4] {'energy'}, dimensions={0} | all-to-all | bytes 262144 | tf_op jit(solution)/shard_map/all_to_all | solution.py:102
  180.0 11.1 %reshape.446 = bf16[16384,1,1,4]{3,2,1,0:T(2,128)(2,1)} reshape(bf16[8,2,4096]{2,1,0:T(2,128)(2,1)S(1)} %all_to_all.24) | data formatting | bytes 262144
  191.1 15.4 %copy.77 = bf16[1,4,1,16384]{3,1,2,0:T(4,128)(2,1)S(1)} copy(bf16[1,4,1,16384]{1,2,0,3:T(2,128)(2,1)} %bitcast.234) | data formatting | bytes 262144 | tf_op jit(solution)/shard_map/all_to_all | solution.py:102
  207.0 0.2 fusion.99
  207.4 0.2 fusion.104
  207.8 0.2 fusion.100
  208.2 0.2 convolution_add_fusion.1
  208.6 0.2 convolution_add_fusion.5
  208.8 0.2 convolution_add_fusion.7
  209.2 0.2 fusion.2
  209.4 0.2 fusion.3
  209.6 0.2 multiply_subtract_fusion
  209.8 0.3 fusion.50
  210.1 0.3 fusion.52
  210.4 0.3 fusion.11
  210.7 0.3 fusion.10
  211.0 7.4 %all_to_all.25 = bf16[1,2,8,2048]{3,1,0,2:T(2,128)(2,1)S(1)} all-to-all(bf16[1,2,8,2048]{3,1,0,2:T(2,128)(2,1)S(1)} %copy.78), channel_id=1, replica_groups=mesh['energy'=8,'cell'=4] {'energy'}, dimensions={2} | all-to-all | bytes 131072 | tf_op jit(solution)/shard_map/all_to_all | solution.py:104
  218.4 0.3 slice_reduce_fusion.1
  218.8 0.2 fusion.43
  219.0 0.2 fusion.47
  219.2 0.2 fusion.35
  219.4 0.2 fusion.33
  219.6 0.2 fusion.45
  219.9 0.2 fusion.41
  220.1 0.2 fusion.21
  220.4 0.2 fusion.20
  220.6 0.7 pad_maximum_fusion.1
  221.4 33.8 %all-reduce.7.cloned.1.call-done = bf16[4,2,1,128,128]{4,3,0,2,1:T(8,128)(2,1)} async-done(((bf16[4,2,1,128,128]{4,3,0,2,1:T(8,128)(2,1)}), bf16[4,2,1,128,128]{4,3,0,2,1:T(8,128)(2,1)}) %all-reduce.7.cloned.1.call-update) | async-done | bytes 262160
  255.2 2.1 dynamic-slice_bitcast_fusion
  257.3 0.6 copy.117
  (29 shorter events, 2.3 us)
Async XLA Ops:
  7.2 49.3 %all-reduce.5.cloned.1.call-start = ((), (), s32[]{:S(2)}) async-start(), calls=%async_computation.2 | async-start | bytes 524288
  18.0 237.2 %all-reduce.7.cloned.1.call-start = ((), (), s32[]{:S(2)}) async-start(), calls=%async_computation.3 | async-start | bytes 524288
  191.1 27.7 %copy-start = (bf16[2,1,4,128,128]{4,3,2,1,0:T(8,128)(2,1)S(1)}, bf16[2,1,4,128,128]{4,3,2,1,0:T(8,128)(2,1)}, u32[]{:S(2)}) copy-start(bf16[2,1,4,128,128]{4,3,2,1,0:T(8,128)(2,1)} %param.6) | copy-start | bytes 786436
Sparse Core Ops, SparseCore 0:
  18.1 38.2 all-reduce.4
  221.5 33.6 all-reduce.6
where the time goes:
time: 266 us; the launch traced here: 265 us
  other arithmetic  94.8 us (36%)
  waiting for transfers between devices  69.6 us (26%)
  local copies, waits for them, and re-layouts  54.4 us (20%)
  blocking collectives  16.4 us (6%)
  matrix products  15.2 us (6%)
  between operations  14.4 us (5%)
    unnamed x1, other arithmetic  90.8 us
    unnamed x4, waiting for transfers between devices  69.6 us
    unnamed x10, local copies, waits for them, and re-layouts  24.5 us
    all_to_all x1, local copies, waits for them, and re-layouts, on_device(): lax.all_to_all(flat, 'energy', split_axis=3, concat_axis=2, tiled=True)  15.4 us
    concatenate x3, local copies, waits for them, and re-layouts, on_device(): both = jnp.concatenate([lesser, greater], axis=1).astype(jnp.bfloat16)  12.9 us
    all_to_all x1, blocking collectives, on_device(): lax.all_to_all(flat, 'energy', split_axis=3, concat_axis=2, tiled=True)  8.95 us
    all_to_all x1, blocking collectives, on_device(): lax.all_to_all(polar, 'energy', split_axis=2, concat_axis=3, tiled=True)  7.4 us
    dot_general x8, matrix products, adjoint_product(): jnp.einsum('eibjc,eidjc->iebd', left, right, preferred_element_type=jnp.f...  5.52 us
  transfers between devices with their start and end apart: 2, of which 2 were waited for; matrix products, arithmetic and copies ran while one was open for 1% of the time, Pallas kernels for 0%

commit v1 on v0

v1 whole, which is shorter than its diff:
```python
import functools
import math

import jax
import jax.numpy as jnp
from jax import lax
from jax.experimental import pallas as pl
from jax.experimental.pallas import tpu as pltpu
from jax.sharding import PartitionSpec as P

VMEM = pltpu.MemorySpace.VMEM
SMEM = pltpu.MemorySpace.SMEM


def call(body, out_shape, spaces):
    outs = out_shape if isinstance(out_shape, (tuple, list)) else (out_shape,)
    out_specs = [pl.BlockSpec(memory_space=VMEM) for _ in outs]
    return pl.pallas_call(
        body,
        out_shape=out_shape,
        in_specs=[pl.BlockSpec(memory_space=space) for space in spaces],
        out_specs=out_specs if isinstance(out_shape, (tuple, list)) else out_specs[0],
    )


def source_matrix(src_re, src_im):
    return jnp.concatenate(
        [
            jnp.concatenate([src_re, src_im], axis=1),
            jnp.concatenate([-src_im, src_re], axis=1),
        ],
        axis=0,
    )


def sandwich_block(block, source):
    half = block.shape[0]
    mid = jnp.dot(block, source, preferred_element_type=jnp.float32).astype(jnp.bfloat16)
    turned = jnp.concatenate([mid[:, half:], -mid[:, :half]], axis=1)
    left = jnp.concatenate([mid, turned], axis=0)
    return lax.dot_general(
        left, block, (((1,), (1,)), ((), ())), preferred_element_type=jnp.float32
    )


def lesser_kernel(coupling, green, sigma, chunks, spectral):
    cell = lax.axis_index("cell")
    owners, cells, _, rows, _ = chunks.shape
    orbitals = owners * rows
    source = source_matrix(sigma[0, 0], sigma[1, 0])
    diag_re = green[0, 0, cell].astype(jnp.float32)
    diag_im = green[1, 0, cell].astype(jnp.float32)
    diff_re = (diag_re - diag_re.T).astype(jnp.bfloat16)
    diff_im = (diag_im + diag_im.T).astype(jnp.bfloat16)
    for owner in range(owners):
        here = slice(owner * rows, (owner + 1) * rows)
        spectral[owner, 0] = diff_re[here]
        spectral[owner, 1] = diff_im[here]
    for i in range(cells):
        block = jnp.concatenate([green[0, 0, i], green[1, 0, i]], axis=1)
        part = sandwich_block(block, source)
        part = (part * coupling[i, cell].astype(jnp.float32)).astype(jnp.bfloat16)
        for owner in range(owners):
            for c in range(2):
                start = c * orbitals + owner * rows
                chunks[owner, i, c] = part[start : start + rows]


def correlate_kernel(chunks, spectral, polar):
    energies, cells = chunks.shape[0], chunks.shape[1]
    scale = 1.0 / math.sqrt(energies)
    lesser, greater = [], []
    for e in range(energies):
        low, high = [], []
        for c in range(2):
            total = chunks[e, 0, c].astype(jnp.float32)
            for j in range(1, cells):
                total = total + chunks[e, j, c].astype(jnp.float32)
            above = total + spectral[e, c].astype(jnp.float32)
            low.append(total.astype(jnp.bfloat16).astype(jnp.float32))
            high.append(above.astype(jnp.bfloat16).astype(jnp.float32))
        lesser.append(low)
        greater.append(high)
    for w in range(energies):
        real = imag = None
        for e in range(energies - w):
            low_re, low_im = lesser[e + w]
            high_re, high_im = greater[e]
            re = low_im * high_re - low_re * high_im
            im = low_re * high_re + low_im * high_im
            real = re if real is None else real + re
            imag = im if imag is None else imag + im
        polar[w, 0] = (real * scale).astype(jnp.bfloat16)
        polar[w, 1] = (imag * -scale).astype(jnp.bfloat16)


def screened_kernel(coupling, screen, rows, polar, partial):
    cell = lax.axis_index("cell")
    owners, _, height, width = rows.shape
    cells = screen.shape[2]
    parts = [rows[:, c].reshape(owners * height, width) for c in range(2)]
    polar[0] = parts[0]
    polar[1] = parts[1]
    source = source_matrix(*parts)
    for i in range(cells):
        block = jnp.concatenate([screen[0, 0, i], screen[1, 0, i]], axis=1)
        part = sandwich_block(block, source)
        part = (part * coupling[i, cell].astype(jnp.float32)).astype(jnp.bfloat16)
        partial[i, 0] = part[:width]
        partial[i, 1] = part[width:]


def on_device(g_retarded, sigma_lesser, w_screened, coupling):
    owners = lax.axis_size("energy")
    cells = lax.axis_size("cell")
    orbitals = sigma_lesser.shape[2]
    rows = orbitals // owners
    half = functools.partial(jax.ShapeDtypeStruct, dtype=jnp.bfloat16)
    chunks, spectral = call(
        lesser_kernel,
        (half((owners, cells, 2, rows, orbitals)), half((owners, 2, rows, orbitals))),
        (SMEM, VMEM, VMEM),
    )(coupling, g_retarded, sigma_lesser)
    spectral = lax.all_to_all(spectral, "energy", 0, 0, tiled=True)
    chunks = lax.all_to_all(
        chunks.reshape(owners * cells, 2, rows, orbitals), ("energy", "cell"), 0, 0, tiled=True
    ).reshape(owners, cells, 2, rows, orbitals)
    polar = call(correlate_kernel, half((owners, 2, rows, orbitals)), (VMEM, VMEM))(
        chunks, spectral
    )
    polar = lax.all_to_all(polar, "energy", 0, 0, tiled=True)
    polar, partial = call(
        screened_kernel,
        (half((2, orbitals, orbitals)), half((cells, 2, orbitals, orbitals))),
        (SMEM, VMEM, VMEM),
    )(coupling, w_screened, polar)
    partial = lax.all_to_all(partial, "cell", 0, 0, tiled=True)
    screened = partial.astype(jnp.float32).sum(axis=0).astype(jnp.bfloat16)
    return (
        polar.reshape(1, 2, 1, orbitals * orbitals),
        screened.reshape(1, 2, 1, orbitals, orbitals),
    )


def solution(mesh):
    return jax.shard_map(
        on_device,
        mesh=mesh,
        in_specs=(
            P(None, "energy", None, None, "cell"),
            P(None, "energy", None, "cell"),
            P(None, "energy", None, None, "cell"),
            P(),
        ),
        out_specs=(P("cell", None, "energy", None), P("cell", None, "energy", None, None)),
        check_vma=False,
    )
```

time: 266 us -> 54.2 us (0.20)
  other arithmetic: 94.8 us -> 0.67 us
  waiting for transfers between devices: 69.6 us -> 8.3 us
  local copies, waits for them, and re-layouts: 54.4 us -> 0.65 us
  blocking collectives: 16.4 us -> 33.7 us
  matrix products: 15.2 us -> 0 us
  between operations: 14.4 us -> 0.65 us
  Pallas kernels: 0 us -> 6.13 us
  starting transfers between devices: 0.08 us -> 3.54 us
    unnamed x1 -> x0, other arithmetic: 90.8 us -> none
    unnamed x4 -> x0, waiting for transfers between devices: 69.6 us -> none
    unnamed x10 -> x2, local copies, waits for them, and re-layouts: 24.5 us -> 0.01 us
    all_to_all x2 -> x3, blocking collectives: 16.4 us -> 33.7 us  [the longest x1 14.4 us: on_device(): lax.all_to_all(chunks.reshape(owners * cells, 2, rows, orbitals), ('energ...]
    all_to_all x1 -> x0, local copies, waits for them, and re-layouts: 15.4 us -> none  [on_device(): lax.all_to_all(flat, 'energy', split_axis=3, concat_axis=2, tiled=True)]
    dot_general x36 -> x0, matrix products: 15.2 us -> none  [the longest x8 5.52 us: adjoint_product(): jnp.einsum('eibjc,eidjc->iebd', left, right, preferred_element_type=jnp.f...]
    concatenate x3 -> x0, local copies, waits for them, and re-layouts: 12.9 us -> none  [on_device(): both = jnp.concatenate([lesser, greater], axis=1).astype(jnp.bfloat16)]
    all_to_all x0 -> x1, waiting for transfers between devices: none -> 8.3 us  [on_device(): partial = lax.all_to_all(partial, 'cell', 0, 0, tiled=True)]
  transfers between devices with their start and end apart: 2 -> 1, of which waited for: 2 -> 1; matrix products, arithmetic and copies ran while one was open for 1% -> 1% of each run, Pallas kernels for 0% -> 0%
where the time goes in v1:
time: 54.2 us; the launch traced here: 53.7 us
  blocking collectives  33.7 us (62%)
  waiting for transfers between devices  8.3 us (15%)
  Pallas kernels  6.13 us (11%)
  starting transfers between devices  3.54 us (7%)
  other arithmetic  0.67 us (1%)
  local copies, waits for them, and re-layouts  0.65 us (1%)
  between operations  0.65 us (1%)
    all_to_all x1, blocking collectives, on_device(): lax.all_to_all(chunks.reshape(owners * cells, 2, rows, orbitals), ('energ...  14.4 us
    all_to_all x1, blocking collectives, on_device(): spectral = lax.all_to_all(spectral, 'energy', 0, 0, tiled=True)  10.3 us
    all_to_all x1, blocking collectives, on_device(): polar = lax.all_to_all(polar, 'energy', 0, 0, tiled=True)  8.97 us
    all_to_all x1, waiting for transfers between devices, on_device(): partial = lax.all_to_all(partial, 'cell', 0, 0, tiled=True)  8.3 us
    all_to_all x1, starting transfers between devices, on_device(): partial = lax.all_to_all(partial, 'cell', 0, 0, tiled=True)  3.54 us
    pallas_call x1, Pallas kernels, on_device(): call(lesser_kernel, (half((owners, cells, 2, rows, orbitals)), half((owne...  2.21 us
    pallas_call x1, Pallas kernels, on_device(): call(screened_kernel, (half((2, orbitals, orbitals)), half((cells, 2, orb...  2.21 us
    pallas_call x1, Pallas kernels, on_device(): call(correlate_kernel, half((owners, 2, rows, orbitals)), (VMEM, VMEM))  1.71 us
  transfers between devices with their start and end apart: 1, of which 1 were waited for; matrix products, arithmetic and copies ran while one was open for 1% of the time, Pallas kernels for 0%

profile of v1, /device:TPU:0, one launch (start us, length us, event | category | flops | bytes accessed | tf_op | source)
XLA Modules:
  0.0 53.7 jit_solution(16879163321424372049)
XLA Ops:
  0.6 2.2 %shard_map.59 = (bf16[8,4,2,16,128]{4,3,2,1,0:T(8,128)(2,1)}, bf16[8,2,16,128]{3,2,1,0:T(8,128)(2,1)}) custom-call(s32[4,4]{1,0:T(4,128)} %coupling.3, bf16[2,1,4,128,128]{4,3,2,1,0:T(8,128)(2,1)} %green.1, bf16[2,1,128,128]{3,2,1,0:T(8,128)(2,1)} %sigma.1), custom_call_target="tpu_custom_call" | custom-call | tf_op jit(solution)/shard_map/pallas_call | solution.py:119
  2.8 10.3 %all_to_all.20.spectral = bf16[8,2,16,128]{3,2,1,0:T(8,128)(2,1)} all-to-all(bf16[8,2,16,128]{3,2,1,0:T(8,128)(2,1)} %get-tuple-element.7), channel_id=1, replica_groups=mesh['energy'=8,'cell'=4] {'energy'}, dimensions={0} | all-to-all | bytes 131072 | tf_op jit(solution)/shard_map/all_to_all | solution.py:124
  13.2 14.4 %all_to_all.21 = bf16[32,2,16,128]{3,2,1,0:T(8,128)(2,1)} all-to-all(bf16[32,2,16,128]{3,2,1,0:T(8,128)(2,1)} %bitcast.4), channel_id=1, replica_groups=mesh['energy'=8,'cell'=4] {'energy','cell'}, dimensions={0} | all-to-all | bytes 524288 | tf_op jit(solution)/shard_map/all_to_all | solution.py:125
  27.6 1.7 %shard_map.60 = bf16[8,2,16,128]{3,2,1,0:T(8,128)(2,1)} custom-call(bf16[8,4,2,16,128]{4,3,2,1,0:T(8,128)(2,1)} %bitcast.3, bf16[8,2,16,128]{3,2,1,0:T(8,128)(2,1)} %all_to_all.20.spectral), custom_call_target="tpu_custom_call" | custom-call | tf_op jit(solution)/shard_map/pallas_call | solution.py:128
  29.3 9.0 %all_to_all.22.rows = bf16[8,2,16,128]{3,2,1,0:T(8,128)(2,1)} all-to-all(bf16[8,2,16,128]{3,2,1,0:T(8,128)(2,1)} %shard_map.60), channel_id=1, replica_groups=mesh['energy'=8,'cell'=4] {'energy'}, dimensions={0} | all-to-all | bytes 131072 | tf_op jit(solution)/shard_map/all_to_all | solution.py:131
  38.3 2.2 %shard_map.61 = (bf16[2,128,128]{2,1,0:T(8,128)(2,1)}, bf16[4,2,128,128]{3,2,1,0:T(8,128)(2,1)}) custom-call(s32[4,4]{1,0:T(4,128)} %coupling.3, bf16[2,1,4,128,128]{4,3,2,1,0:T(8,128)(2,1)} %screen.1, bf16[8,2,16,128]{3,2,1,0:T(8,128)(2,1)} %all_to_all.22.rows), custom_call_target="tpu_custom_call" | custom-call | tf_op jit(solution)/shard_map/pallas_call | solution.py:132
  40.5 0.0 copy-start
  40.5 3.5 %all-to-all-start.3 = ((bf16[4,2,128,128]{3,2,1,0:T(8,128)(2,1)}), bf16[4,2,128,128]{3,2,1,0:T(8,128)(2,1)S(1)}, u32[]{:S(2)}, u32[]{:S(2)}) async-start(bf16[4,2,128,128]{3,2,1,0:T(8,128)(2,1)} %get-tuple-element.9), calls=%async_computation.3 | async-start | bytes 524288 | tf_op jit(solution)/shard_map/all_to_all | solution.py:137
  44.0 0.0 copy-done
  44.0 0.7 %reshape.18 = bf16[1,2,1,16384]{3,1,2,0:T(2,128)(2,1)} reshape(bf16[2,128,128]{2,1,0:T(8,128)(2,1)S(1)} %copy-done) | data formatting | bytes 131072 | tf_op jit(solution)/shard_map/reshape | solution.py:140
  44.7 8.3 %all-to-all-done.3 = bf16[4,2,128,128]{3,2,1,0:T(8,128)(2,1)S(1)} async-done(((bf16[4,2,128,128]{3,2,1,0:T(8,128)(2,1)}), bf16[4,2,128,128]{3,2,1,0:T(8,128)(2,1)S(1)}, u32[]{:S(2)}, u32[]{:S(2)}) %all-to-all-start.3) | async-done | bytes 262176 | tf_op jit(solution)/shard_map/all_to_all | solution.py:137
  53.0 0.7 %reduce_sum.12 = bf16[2,128,128]{2,1,0:T(8,128)(2,1)} reduce(bf16[4,2,128,128]{3,2,1,0:T(8,128)(2,1)S(1)} %all-to-all-done.3, bf16[]{:T(256)} %constant.2.clone.1), dimensions={0}, to_apply=%region_0.0 | reduce | flops 98304 | bytes 327682 | tf_op jit(solution)/shard_map/reduce_sum | solution.py:138
Async XLA Ops:
  40.5 3.5 %copy-start = (bf16[2,128,128]{2,1,0:T(8,128)(2,1)S(1)}, bf16[2,128,128]{2,1,0:T(8,128)(2,1)}, u32[]{:S(2)}) copy-start(bf16[2,128,128]{2,1,0:T(8,128)(2,1)} %get-tuple-element.8) | copy-start | bytes 196612
  40.5 12.5 %all-to-all-start.3 = ((bf16[4,2,128,128]{3,2,1,0:T(8,128)(2,1)}), bf16[4,2,128,128]{3,2,1,0:T(8,128)(2,1)S(1)}, u32[]{:S(2)}, u32[]{:S(2)}) async-start(bf16[4,2,128,128]{3,2,1,0:T(8,128)(2,1)} %get-tuple-element.9), calls=%async_computation.3 | async-start | bytes 524288 | tf_op jit(solution)/shard_map/all_to_all | solution.py:137

commit v2 on v1

v2 whole, which is shorter than its diff:
```python
import functools
import math

import jax
import jax.numpy as jnp
from jax import lax
from jax.experimental import pallas as pl
from jax.experimental.pallas import tpu as pltpu
from jax.sharding import PartitionSpec as P


VMEM = pltpu.MemorySpace.VMEM
SMEM = pltpu.MemorySpace.SMEM
HBM = pltpu.MemorySpace.HBM


def call(body, out_shape, spaces, *operands, scratch=()):
    several = isinstance(out_shape, (tuple, list))
    outs = out_shape if several else (out_shape,)
    held = sum(array.size * array.dtype.itemsize for array in (*operands, *outs))
    out_specs = [pl.BlockSpec(memory_space=VMEM) for _ in outs]
    return pl.pallas_call(
        body,
        out_shape=out_shape,
        in_specs=[pl.BlockSpec(memory_space=space) for space in spaces],
        out_specs=out_specs if several else out_specs[0],
        scratch_shapes=scratch,
        compiler_params=pltpu.CompilerParams(vmem_limit_bytes=2 * held + (4 << 20)),
    )(*operands)


def source_matrix(src_re, src_im):
    return jnp.concatenate(
        [
            jnp.concatenate([src_re, src_im], axis=1),
            jnp.concatenate([-src_im, src_re], axis=1),
        ],
        axis=0,
    )


def sandwich_block(block, source):
    half = block.shape[0]
    mid = jnp.dot(block, source, preferred_element_type=jnp.float32).astype(jnp.bfloat16)
    turned = jnp.concatenate([mid[:, half:], -mid[:, :half]], axis=1)
    left = jnp.concatenate([mid, turned], axis=0)
    return lax.dot_general(
        left, block, (((1,), (1,)), ((), ())), preferred_element_type=jnp.float32
    )


def prepare_kernel(coupling, screen, green, spectral, *rest):
    *blocks, diagonal, couple, sems = rest
    energy = lax.axis_index("energy")
    cell = lax.axis_index("cell")
    cells = screen.shape[2]
    owners, _, rows, _ = spectral.shape
    copies = [
        pltpu.make_async_copy(green.at[:, 0, cell], diagonal, sems.at[cells]),
        pltpu.make_async_copy(coupling, couple, sems.at[cells + 1]),
    ]
    for shift in range(cells):
        row = lax.rem(cell + shift, cells)
        copies.append(pltpu.make_async_copy(screen.at[:, 0, row], blocks[shift], sems.at[shift]))
    for copy in copies:
        copy.start()
    copies[0].wait()
    diag_re = diagonal[0].astype(jnp.float32)
    diag_im = diagonal[1].astype(jnp.float32)
    difference = (diag_re - diag_re.T, diag_im + diag_im.T)
    for owner in range(owners):
        for c in range(2):
            here = difference[c][owner * rows : (owner + 1) * rows]
            spectral[owner ^ energy, c] = here.astype(jnp.bfloat16)
    copies[1].wait()
    for shift in range(cells):
        copies[2 + shift].wait()
        weight = couple[lax.rem(cell + shift, cells), cell].astype(jnp.float32)
        blocks[shift][...] = (blocks[shift][...].astype(jnp.float32) * weight).astype(jnp.bfloat16)


def lesser_kernel(coupling, green, sigma, chunks):
    cell = lax.axis_index("cell")
    owners, cells, _, rows, _ = chunks.shape
    orbitals = owners * rows
    matrix = source_matrix(sigma[0, 0], sigma[1, 0])
    for i in range(cells):
        block = jnp.concatenate([green[0, 0, i], green[1, 0, i]], axis=1)
        part = sandwich_block(block, matrix)
        part = (part * coupling[i, cell].astype(jnp.float32)).astype(jnp.bfloat16)
        for owner in range(owners):
            for c in range(2):
                start = c * orbitals + owner * rows
                chunks[owner, i, c] = part[start : start + rows]


def correlate_kernel(chunks, spectral, polar):
    energies, cells = chunks.shape[0], chunks.shape[1]
    here = lax.axis_index("energy")
    scale = 1.0 / math.sqrt(energies)
    lesser, greater = [], []
    for e in range(energies):
        low, high = [], []
        for c in range(2):
            total = chunks[e, 0, c].astype(jnp.float32)
            for j in range(1, cells):
                total = total + chunks[e, j, c].astype(jnp.float32)
            above = total + spectral[here ^ e, c].astype(jnp.float32)
            low.append(total.astype(jnp.bfloat16).astype(jnp.float32))
            high.append(above.astype(jnp.bfloat16).astype(jnp.float32))
        lesser.append(low)
        greater.append(high)
    for w in range(energies):
        real = imag = None
        for e in range(energies - w):
            low_re, low_im = lesser[e + w]
            high_re, high_im = greater[e]
            re = low_im * high_re - low_re * high_im
            im = low_re * high_re + low_im * high_im
            real = re if real is None else real + re
            imag = im if imag is None else imag + im
        real = (real * scale).astype(jnp.bfloat16)
        imag = (imag * -scale).astype(jnp.bfloat16)
        for i in range(cells):
            polar[w, i, 0] = real
            polar[w, i, 1] = imag


def screened_kernel(_, rows, *rest):
    *blocks, polar, result = rest
    cell = lax.axis_index("cell")
    owners, cells, _, height, width = rows.shape
    total = None
    for shift in range(cells):
        j = lax.rem(cell + cells - shift, cells)
        parts = [rows[:, j, c].reshape(owners * height, width) for c in range(2)]
        if not shift:
            polar[0] = parts[0]
            polar[1] = parts[1]
        block = jnp.concatenate([blocks[shift][0], blocks[shift][1]], axis=1)
        part = sandwich_block(block, source_matrix(*parts))
        part = part.astype(jnp.bfloat16).astype(jnp.float32)
        total = part if total is None else total + part
    total = total.astype(jnp.bfloat16)
    result[0] = total[:width]
    result[1] = total[width:]


def spread_spectral(spectral, owners):
    held = [spectral[distance] for distance in range(owners)]
    bit = 1
    while bit < owners:
        moved = [distance for distance in range(owners) if distance & bit]
        sent = jnp.stack([held[distance] for distance in moved])
        got = lax.ppermute(sent, "energy", [(k, k ^ bit) for k in range(owners)])
        for place, distance in enumerate(moved):
            held[distance] = got[place]
        bit *= 2
    return jnp.stack(held)


def on_device(g_retarded, sigma_lesser, w_screened, coupling):
    owners = lax.axis_size("energy")
    cells = lax.axis_size("cell")
    orbitals = sigma_lesser.shape[2]
    rows = orbitals // owners
    half = functools.partial(jax.ShapeDtypeStruct, dtype=jnp.bfloat16)
    square = half((2, orbitals, orbitals))
    spectral, own, *leaving = call(
        prepare_kernel,
        (half((owners, 2, rows, orbitals)),) + (square,) * cells,
        (HBM, HBM, HBM),
        pltpu.with_memory_space_constraint(coupling, HBM),
        pltpu.with_memory_space_constraint(w_screened, HBM),
        pltpu.with_memory_space_constraint(g_retarded, HBM),
        scratch=(
            pltpu.VMEM(square.shape, square.dtype),
            pltpu.SMEM(coupling.shape, coupling.dtype),
            pltpu.SemaphoreType.DMA((cells + 2,)),
        ),
    )
    arrived = []
    for shift, block in enumerate(leaving, 1):
        pairs = [(k, (k + shift) % cells) for k in range(cells)]
        arrived.append(lax.ppermute(block, "cell", pairs))
    spectral = spread_spectral(spectral, owners)
    chunks = call(
        lesser_kernel,
        half((owners, cells, 2, rows, orbitals)),
        (SMEM, VMEM, VMEM),
        coupling,
        g_retarded,
        sigma_lesser,
    )
    chunks = lax.all_to_all(
        chunks.reshape(owners * cells, 2, rows, orbitals), ("energy", "cell"), 0, 0, tiled=True
    ).reshape(owners, cells, 2, rows, orbitals)
    polar = call(
        correlate_kernel,
        half((owners, cells, 2, rows, orbitals)),
        (VMEM, VMEM),
        chunks,
        spectral,
    )
    polar = lax.all_to_all(
        polar.reshape(owners * cells, 2, rows, orbitals), ("energy", "cell"), 0, 0, tiled=True
    ).reshape(owners, cells, 2, rows, orbitals)
    anchor = polar[0, 0, 0] * 2
    polar, screened = call(
        screened_kernel,
        (square, square),
        (HBM,) + (VMEM,) * (2 + len(arrived)),
        anchor,
        polar,
        own,
        *arrived,
    )
    return (
        polar.reshape(1, 2, 1, orbitals * orbitals),
        screened.reshape(1, 2, 1, orbitals, orbitals),
    )


def solution(mesh):
    return jax.shard_map(
        on_device,
        mesh=mesh,
        in_specs=(
            P(None, "energy", None, None, "cell"),
            P(None, "energy", None, "cell"),
            P(None, "energy", None, None, "cell"),
            P(),
        ),
        out_specs=(P("cell", None, "energy", None), P("cell", None, "energy", None, None)),
        check_vma=False,
    )
```

time: 54.2 us -> 42.9 us (0.79)
  blocking collectives: 33.7 us -> 0 us
  starting transfers between devices: 3.54 us -> 18.5 us
  waiting for transfers between devices: 8.3 us -> 17.7 us
  Pallas kernels: 6.13 us -> 4.91 us
  other arithmetic: 0.67 us -> 0.03 us
    all_to_all x3 -> x0, blocking collectives: 33.7 us -> none  [the longest x1 14.4 us: on_device(): lax.all_to_all(chunks.reshape(owners * cells, 2, rows, orbitals), ('energ...]
    ppermute x0 -> x6, starting transfers between devices: none -> 10.9 us  [the longest x3 5.65 us: on_device(): arrived.append(lax.ppermute(block, 'cell', pairs))]
    ppermute x0 -> x6, waiting for transfers between devices: none -> 7.23 us  [the longest x3 3.87 us: on_device(): arrived.append(lax.ppermute(block, 'cell', pairs))]
    all_to_all x1 -> x2, starting transfers between devices: 3.54 us -> 7.62 us  [the longest x1 4.96 us: on_device(): lax.all_to_all(chunks.reshape(owners * cells, 2, rows, orbitals), ('energ...]
    all_to_all x1 -> x2, waiting for transfers between devices: 8.3 us -> 10.5 us  [the longest x1 5.84 us: on_device(): lax.all_to_all(chunks.reshape(owners * cells, 2, rows, orbitals), ('energ...]
    pallas_call x3 -> x4, Pallas kernels: 6.13 us -> 4.91 us  [call(): pl.pallas_call(body, out_shape=out_shape, in_specs=[pl.BlockSpec(memory_s...]
    reduce_sum x1 -> x0, other arithmetic: 0.67 us -> none  [on_device(): screened = partial.astype(jnp.float32).sum(axis=0).astype(jnp.bfloat16)]
  transfers between devices with their start and end apart: 1 -> 8, of which waited for: 1 -> 6; matrix products, arithmetic and copies ran while one was open for 1% -> 0% of each run, Pallas kernels for 0% -> 4%
where the time goes in v2:
time: 42.9 us; the launch traced here: 42.6 us
  starting transfers between devices  18.5 us (43%)
  waiting for transfers between devices  17.7 us (41%)
  Pallas kernels  4.91 us (11%)
  between operations  0.73 us (2%)
  local copies, waits for them, and re-layouts  0.68 us (2%)
    all_to_all x1, waiting for transfers between devices, on_device(): lax.all_to_all(chunks.reshape(owners * cells, 2, rows, orbitals), ('energ...  5.84 us
    ppermute x3, starting transfers between devices, on_device(): arrived.append(lax.ppermute(block, 'cell', pairs))  5.65 us
    ppermute x3, starting transfers between devices, spread_spectral(): got = lax.ppermute(sent, 'energy', [(k, k ^ bit) for k in range(owners)])  5.28 us
    all_to_all x1, starting transfers between devices, on_device(): lax.all_to_all(chunks.reshape(owners * cells, 2, rows, orbitals), ('energ...  4.96 us
    pallas_call x4, Pallas kernels, call(): pl.pallas_call(body, out_shape=out_shape, in_specs=[pl.BlockSpec(memory_s...  4.91 us
    all_to_all x1, waiting for transfers between devices, on_device(): lax.all_to_all(polar.reshape(owners * cells, 2, rows, orbitals), ('energy...  4.61 us
    ppermute x3, waiting for transfers between devices, on_device(): arrived.append(lax.ppermute(block, 'cell', pairs))  3.87 us
    ppermute x3, waiting for transfers between devices, spread_spectral(): got = lax.ppermute(sent, 'energy', [(k, k ^ bit) for k in range(owners)])  3.36 us
  transfers between devices with their start and end apart: 8, of which 6 were waited for; matrix products, arithmetic and copies ran while one was open for 0% of the time, Pallas kernels for 4%

profile of v2, /device:TPU:0, one launch (start us, length us, event | category | flops | bytes accessed | tf_op | source)
XLA Modules:
  0.0 42.6 jit_solution(5179108979344736677)
XLA Ops:
  0.6 1.1 %shard_map.60 = (bf16[8,2,16,128]{3,2,1,0:T(8,128)(2,1)S(1)}, bf16[2,128,128]{2,1,0:T(8,128)(2,1)S(1)}, bf16[2,128,128]{2,1,0:T(8,128)(2,1)S(1)}, bf16[2,128,128...) custom-call(s32[4,4]{1,0:T(4,128)} %coupling.3, bf16[2,1,4,128,128]{4,3,2,1,0:T(8,128)(2,1)} %screen.1, ...), custom_call_target="tpu_custom_call" | custom-call | tf_op jit(solution)/shard_map/pallas_call | solution.py:22
  1.7 0.0 copy-start
  1.8 0.0 copy-start.1
  1.8 0.6 %collective-permute-start = (bf16[4,2,16,128]{3,2,1,0:T(8,128)(2,1)S(1)}, bf16[4,2,16,128]{3,2,1,0:T(8,128)(2,1)S(1)}, u32[]{:S(2)}, u32[]{:S(2)}) collective-permute-start(bf16[4,2,16,128]{3,2,1,0:T(8,128)(2,1)S(1)} %pad_maximum_fusion.1), channel_id=1, source_target_pairs={{0,4},{4,0},{8,12},{12,8},{16,20},{20,16},{24,28},{28,24},{1,5},{5... | collective-permute-start | bytes 98312 | tf_op jit(solution)/shard_map/ppermute | solution.py:155
  2.3 0.9 %collective-permute-done = bf16[4,2,16,128]{3,2,1,0:T(8,128)(2,1)S(1)} collective-permute-done((bf16[4,2,16,128]{3,2,1,0:T(8,128)(2,1)S(1)}, bf16[4,2,16,128]{3,2,1,0:T(8,128)(2,1)S(1)}, u32[]{:S(2)}, u32[]{:S(2)}) %collective-permute-start) | collective-permute-done | bytes 32800 | tf_op jit(solution)/shard_map/ppermute | solution.py:155
  3.2 0.0 copy-start.2
  3.2 2.9 %collective-permute-start.1 = (bf16[4,2,16,128]{3,2,1,0:T(8,128)(2,1)S(1)}, bf16[4,2,16,128]{3,2,1,0:T(8,128)(2,1)S(1)}, u32[]{:S(2)}, u32[]{:S(2)}) collective-permute-start(bf16[4,2,16,128]{3,2,1,0:T(8,128)(2,1)S(1)} %pad_maximum_fusion.2), channel_id=1, source_target_pairs={{0,8},{4,12},{8,0},{12,4},{16,24},{20,28},{24,16},{28,20},{1,9},{5... | collective-permute-start | bytes 98312 | tf_op jit(solution)/shard_map/ppermute | solution.py:155
  6.1 0.0 copy-done
  6.1 0.0 copy-done.1
  6.1 0.0 copy-done.2
  6.1 1.8 %shard_map.59 = bf16[8,4,2,16,128]{4,3,2,1,0:T(8,128)(2,1)} custom-call(s32[4,4]{1,0:T(4,128)S(1)} %copy-done.2, bf16[2,1,4,128,128]{4,3,2,1,0:T(8,128)(2,1)S(1)} %copy-done, bf16[2,1,128,128]{3,2,1,0:T(8,128)(2,1)S(1)} %copy-done.1), custom_call_target="tpu_custom_call" | custom-call | tf_op jit(solution)/shard_map/pallas_call | solution.py:22
  7.9 5.0 %all-to-all-start = ((bf16[32,2,16,128]{3,2,1,0:T(8,128)(2,1)}), bf16[32,2,16,128]{3,2,1,0:T(8,128)(2,1)S(1)}, u32[]{:S(2)}, u32[]{:S(2)}) async-start(bf16[32,2,16,128]{3,2,1,0:T(8,128)(2,1)} %bitcast), calls=%async_computation | async-start | bytes 524288 | tf_op jit(solution)/shard_map/all_to_all | solution.py:195
  12.9 0.0 collective-permute-done.1
  12.9 1.8 %collective-permute-start.2 = (bf16[4,2,16,128]{3,2,1,0:T(8,128)(2,1)S(1)}, bf16[4,2,16,128]{3,2,1,0:T(8,128)(2,1)S(1)}, u32[]{:S(2)}, u32[]{:S(2)}) collective-permute-start(bf16[4,2,16,128]{3,2,1,0:T(8,128)(2,1)S(1)} %pad_maximum_fusion.3), channel_id=1, source_target_pairs={{0,16},{4,20},{8,24},{12,28},{16,0},{20,4},{24,8},{28,12},{1,17},{... | collective-permute-start | bytes 98312 | tf_op jit(solution)/shard_map/ppermute | solution.py:155
  14.8 2.5 %collective-permute-done.2 = bf16[4,2,16,128]{3,2,1,0:T(8,128)(2,1)S(1)} collective-permute-done((bf16[4,2,16,128]{3,2,1,0:T(8,128)(2,1)S(1)}, bf16[4,2,16,128]{3,2,1,0:T(8,128)(2,1)S(1)}, u32[]{:S(2)}, u32[]{:S(2)}) %collective-permute-start.2) | collective-permute-done | bytes 32800 | tf_op jit(solution)/shard_map/ppermute | solution.py:155
  17.3 5.8 %all-to-all-done = bf16[32,2,16,128]{3,2,1,0:T(8,128)(2,1)S(1)} async-done(((bf16[32,2,16,128]{3,2,1,0:T(8,128)(2,1)}), bf16[32,2,16,128]{3,2,1,0:T(8,128)(2,1)S(1)}, u32[]{:S(2)}, u32[]{:S(2)}) %all-to-all-start) | async-done | bytes 262176 | tf_op jit(solution)/shard_map/all_to_all | solution.py:195
  23.1 0.8 %shard_map.61 = bf16[8,4,2,16,128]{4,3,2,1,0:T(8,128)(2,1)} custom-call(bf16[8,4,2,16,128]{4,3,2,1,0:T(8,128)(2,1)S(1)} %bitcast.11, bf16[8,2,16,128]{3,2,1,0:T(8,128)(2,1)S(1)} %pad_maximum_fusion.spectral), custom_call_target="tpu_custom_call" | custom-call | tf_op jit(solution)/shard_map/pallas_call | solution.py:22
  23.9 2.7 %all-to-all-start.1 = ((bf16[32,2,16,128]{3,2,1,0:T(8,128)(2,1)}), bf16[32,2,16,128]{3,2,1,0:T(8,128)(2,1)S(1)}, u32[]{:S(2)}, u32[]{:S(2)}) async-start(bf16[32,2,16,128]{3,2,1,0:T(8,128)(2,1)} %bitcast.2), calls=%async_computation.1 | async-start | bytes 524288 | tf_op jit(solution)/shard_map/all_to_all | solution.py:205
  26.6 1.8 %collective-permute-start.3 = (bf16[2,128,128]{2,1,0:T(8,128)(2,1)S(1)}, bf16[2,128,128]{2,1,0:T(8,128)(2,1)S(1)}, u32[]{:S(2)}, u32[]{:S(2)}) collective-permute-start(bf16[2,128,128]{2,1,0:T(8,128)(2,1)S(1)} %get-tuple-element.11), channel_id=1, source_target_pairs={{0,1},{1,2},{2,3},{3,0},{4,5},{5,6},{6,7},{7,4},{8,9},{9,10},{10,1... | collective-permute-start | bytes 196616 | tf_op jit(solution)/shard_map/ppermute | solution.py:185
  28.4 2.4 %collective-permute-start.4 = (bf16[2,128,128]{2,1,0:T(8,128)(2,1)S(1)}, bf16[2,128,128]{2,1,0:T(8,128)(2,1)S(1)}, u32[]{:S(2)}, u32[]{:S(2)}) collective-permute-start(bf16[2,128,128]{2,1,0:T(8,128)(2,1)S(1)} %get-tuple-element.12), channel_id=1, source_target_pairs={{0,2},{1,3},{2,0},{3,1},{4,6},{5,7},{6,4},{7,5},{8,10},{9,11},{10,... | collective-permute-start | bytes 196616 | tf_op jit(solution)/shard_map/ppermute | solution.py:185
  30.8 1.4 %collective-permute-start.5 = (bf16[2,128,128]{2,1,0:T(8,128)(2,1)S(1)}, bf16[2,128,128]{2,1,0:T(8,128)(2,1)S(1)}, u32[]{:S(2)}, u32[]{:S(2)}) collective-permute-start(bf16[2,128,128]{2,1,0:T(8,128)(2,1)S(1)} %get-tuple-element.13), channel_id=1, source_target_pairs={{0,3},{1,0},{2,1},{3,2},{4,7},{5,4},{6,5},{7,6},{8,11},{9,8},{10,9... | collective-permute-start | bytes 196616 | tf_op jit(solution)/shard_map/ppermute | solution.py:185
  32.3 4.6 %all-to-all-done.1 = bf16[32,2,16,128]{3,2,1,0:T(8,128)(2,1)S(1)} async-done(((bf16[32,2,16,128]{3,2,1,0:T(8,128)(2,1)}), bf16[32,2,16,128]{3,2,1,0:T(8,128)(2,1)S(1)}, u32[]{:S(2)}, u32[]{:S(2)}) %all-to-all-start.1) | async-done | bytes 262176 | tf_op jit(solution)/shard_map/all_to_all | solution.py:205
  36.9 0.6 %collective-permute-done.3.rest_1_ = bf16[2,128,128]{2,1,0:T(8,128)(2,1)S(1)} collective-permute-done((bf16[2,128,128]{2,1,0:T(8,128)(2,1)S(1)}, bf16[2,128,128]{2,1,0:T(8,128)(2,1)S(1)}, u32[]{:S(2)}, u32[]{:S(2)}) %collective-permute-start.3) | collective-permute-done | bytes 65568 | tf_op jit(solution)/shard_map/ppermute | solution.py:185
  37.5 3.3 %collective-permute-done.4.rest_2_ = bf16[2,128,128]{2,1,0:T(8,128)(2,1)S(1)} collective-permute-done((bf16[2,128,128]{2,1,0:T(8,128)(2,1)S(1)}, bf16[2,128,128]{2,1,0:T(8,128)(2,1)S(1)}, u32[]{:S(2)}, u32[]{:S(2)}) %collective-permute-start.4) | collective-permute-done | bytes 65568 | tf_op jit(solution)/shard_map/ppermute | solution.py:185
  40.7 0.0 collective-permute-done.5.rest_3_
  40.7 1.2 %shard_map.62 = (bf16[2,128,128]{2,1,0:T(8,128)(2,1)S(1)}, bf16[2,128,128]{2,1,0:T(8,128)(2,1)}) custom-call(bf16[16,128]{1,0:T(8,128)(2,1)S(1)} %fusion._, bf16[8,4,2,16,128]{4,3,2,1,0:T(8,128)(2,1)S(1)} %bitcast.10, bf16[2,128,128]{2,1,0:T(8,128)(2,1)S(1)} %get-tuple-element.10.rest_0_, bf16[2,128,128]{2,1,0:T(8,128)(2,1)S(1)} %collective-permute-done.3.rest_1_, ...), custom_call_target="tpu_custom_call" | custom-call | tf_op jit(solution)/shard_map/pallas_call | solution.py:22
  41.9 0.7 %reshape.28 = bf16[1,2,1,16384]{3,1,2,0:T(2,128)(2,1)} reshape(bf16[2,128,128]{2,1,0:T(8,128)(2,1)S(1)} %get-tuple-element.14) | data formatting | bytes 131072 | tf_op jit(solution)/shard_map/reshape | solution.py:219
  (8 shorter events, 0.1 us)
Async XLA Ops:
  1.7 4.4 %copy-start = (bf16[2,1,4,128,128]{4,3,2,1,0:T(8,128)(2,1)S(1)}, bf16[2,1,4,128,128]{4,3,2,1,0:T(8,128)(2,1)}, u32[]{:S(2)}) copy-start(bf16[2,1,4,128,128]{4,3,2,1,0:T(8,128)(2,1)} %green.3) | copy-start | bytes 786436
  1.8 4.3 %copy-start.1 = (bf16[2,1,128,128]{3,2,1,0:T(8,128)(2,1)S(1)}, bf16[2,1,128,128]{3,2,1,0:T(8,128)(2,1)}, u32[]{:S(2)}) copy-start(bf16[2,1,128,128]{3,2,1,0:T(8,128)(2,1)} %sigma.1) | copy-start | bytes 196612
  1.8 1.4 %collective-permute-start = (bf16[4,2,16,128]{3,2,1,0:T(8,128)(2,1)S(1)}, bf16[4,2,16,128]{3,2,1,0:T(8,128)(2,1)S(1)}, u32[]{:S(2)}, u32[]{:S(2)}) collective-permute-start(bf16[4,2,16,128]{3,2,1,0:T(8,128)(2,1)S(1)} %pad_maximum_fusion.1), channel_id=1, source_target_pairs={{0,4},{4,0},{8,12},{12,8},{16,20},{20,16},{24,28},{28,24},{1,5},{5... | collective-permute-start | bytes 98312 | tf_op jit(solution)/shard_map/ppermute | solution.py:155
  3.2 2.9 %copy-start.2 = (s32[4,4]{1,0:T(4,128)S(1)}, s32[4,4]{1,0:T(4,128)}, u32[]{:S(2)}) copy-start(s32[4,4]{1,0:T(4,128)} %coupling.3) | copy-start | bytes 196
  3.2 9.7 %collective-permute-start.1 = (bf16[4,2,16,128]{3,2,1,0:T(8,128)(2,1)S(1)}, bf16[4,2,16,128]{3,2,1,0:T(8,128)(2,1)S(1)}, u32[]{:S(2)}, u32[]{:S(2)}) collective-permute-start(bf16[4,2,16,128]{3,2,1,0:T(8,128)(2,1)S(1)} %pad_maximum_fusion.2), channel_id=1, source_target_pairs={{0,8},{4,12},{8,0},{12,4},{16,24},{20,28},{24,16},{28,20},{1,9},{5... | collective-permute-start | bytes 98312 | tf_op jit(solution)/shard_map/ppermute | solution.py:155
  7.9 15.2 %all-to-all-start = ((bf16[32,2,16,128]{3,2,1,0:T(8,128)(2,1)}), bf16[32,2,16,128]{3,2,1,0:T(8,128)(2,1)S(1)}, u32[]{:S(2)}, u32[]{:S(2)}) async-start(bf16[32,2,16,128]{3,2,1,0:T(8,128)(2,1)} %bitcast), calls=%async_computation | async-start | bytes 524288 | tf_op jit(solution)/shard_map/all_to_all | solution.py:195
  12.9 4.3 %collective-permute-start.2 = (bf16[4,2,16,128]{3,2,1,0:T(8,128)(2,1)S(1)}, bf16[4,2,16,128]{3,2,1,0:T(8,128)(2,1)S(1)}, u32[]{:S(2)}, u32[]{:S(2)}) collective-permute-start(bf16[4,2,16,128]{3,2,1,0:T(8,128)(2,1)S(1)} %pad_maximum_fusion.3), channel_id=1, source_target_pairs={{0,16},{4,20},{8,24},{12,28},{16,0},{20,4},{24,8},{28,12},{1,17},{... | collective-permute-start | bytes 98312 | tf_op jit(solution)/shard_map/ppermute | solution.py:155
  23.9 12.9 %all-to-all-start.1 = ((bf16[32,2,16,128]{3,2,1,0:T(8,128)(2,1)}), bf16[32,2,16,128]{3,2,1,0:T(8,128)(2,1)S(1)}, u32[]{:S(2)}, u32[]{:S(2)}) async-start(bf16[32,2,16,128]{3,2,1,0:T(8,128)(2,1)} %bitcast.2), calls=%async_computation.1 | async-start | bytes 524288 | tf_op jit(solution)/shard_map/all_to_all | solution.py:205
  26.6 10.9 %collective-permute-start.3 = (bf16[2,128,128]{2,1,0:T(8,128)(2,1)S(1)}, bf16[2,128,128]{2,1,0:T(8,128)(2,1)S(1)}, u32[]{:S(2)}, u32[]{:S(2)}) collective-permute-start(bf16[2,128,128]{2,1,0:T(8,128)(2,1)S(1)} %get-tuple-element.11), channel_id=1, source_target_pairs={{0,1},{1,2},{2,3},{3,0},{4,5},{5,6},{6,7},{7,4},{8,9},{9,10},{10,1... | collective-permute-start | bytes 196616 | tf_op jit(solution)/shard_map/ppermute | solution.py:185
  28.4 12.3 %collective-permute-start.4 = (bf16[2,128,128]{2,1,0:T(8,128)(2,1)S(1)}, bf16[2,128,128]{2,1,0:T(8,128)(2,1)S(1)}, u32[]{:S(2)}, u32[]{:S(2)}) collective-permute-start(bf16[2,128,128]{2,1,0:T(8,128)(2,1)S(1)} %get-tuple-element.12), channel_id=1, source_target_pairs={{0,2},{1,3},{2,0},{3,1},{4,6},{5,7},{6,4},{7,5},{8,10},{9,11},{10,... | collective-permute-start | bytes 196616 | tf_op jit(solution)/shard_map/ppermute | solution.py:185
  30.8 9.9 %collective-permute-start.5 = (bf16[2,128,128]{2,1,0:T(8,128)(2,1)S(1)}, bf16[2,128,128]{2,1,0:T(8,128)(2,1)S(1)}, u32[]{:S(2)}, u32[]{:S(2)}) collective-permute-start(bf16[2,128,128]{2,1,0:T(8,128)(2,1)S(1)} %get-tuple-element.13), channel_id=1, source_target_pairs={{0,3},{1,0},{2,1},{3,2},{4,7},{5,4},{6,5},{7,6},{8,11},{9,8},{10,9... | collective-permute-start | bytes 196616 | tf_op jit(solution)/shard_map/ppermute | solution.py:185

commit v3 on v2

--- a/solution.py
+++ b/solution.py
@@ -10,15 +10,16 @@
 
 
 VMEM = pltpu.MemorySpace.VMEM
-SMEM = pltpu.MemorySpace.SMEM
 HBM = pltpu.MemorySpace.HBM
 
 
-def call(body, out_shape, spaces, *operands, scratch=()):
+def call(body, out_shape, spaces, *operands, scratch=(), out_spaces=None):
     several = isinstance(out_shape, (tuple, list))
     outs = out_shape if several else (out_shape,)
     held = sum(array.size * array.dtype.itemsize for array in (*operands, *outs))
-    out_specs = [pl.BlockSpec(memory_space=VMEM) for _ in outs]
+    out_specs = [
+        pl.BlockSpec(memory_space=space) for space in out_spaces or (VMEM,) * len(outs)
+    ]
     return pl.pallas_call(
         body,
         out_shape=out_shape,
@@ -29,6 +30,12 @@
     )(*operands)
 
 
+def partner(cell, shift, cells):
+    if cells & (cells - 1) == 0:
+        return cell ^ abs(shift)
+    return (cell + shift + cells) % cells
+
+
 def source_matrix(src_re, src_im):
     return jnp.concatenate(
         [
@@ -42,56 +49,59 @@
 def sandwich_block(block, source):
     half = block.shape[0]
     mid = jnp.dot(block, source, preferred_element_type=jnp.float32).astype(jnp.bfloat16)
-    turned = jnp.concatenate([mid[:, half:], -mid[:, :half]], axis=1)
-    left = jnp.concatenate([mid, turned], axis=0)
-    return lax.dot_general(
-        left, block, (((1,), (1,)), ((), ())), preferred_element_type=jnp.float32
-    )
-
-
-def prepare_kernel(coupling, screen, green, spectral, *rest):
-    *blocks, diagonal, couple, sems = rest
+    turned = jnp.concatenate([-block[:, half:], block[:, :half]], axis=1)
+    right = jnp.concatenate([block, turned], axis=0)
+    both = lax.dot_general(
+        mid, right, (((1,), (1,)), ((), ())), preferred_element_type=jnp.float32
+    )
+    return jnp.concatenate([both[:, :half], both[:, half:]], axis=0)
+
+
+def lesser_kernel(coupling, screen, green, sigma, chunks, spectral, *rest):
+    cells = screen.shape[2]
+    blocks, (couple, source, columns, placed, arrivals, departures) = rest[:cells], rest[cells:]
     energy = lax.axis_index("energy")
     cell = lax.axis_index("cell")
-    cells = screen.shape[2]
-    owners, _, rows, _ = spectral.shape
+    owners, _, rows, orbitals = spectral.shape
     copies = [
-        pltpu.make_async_copy(green.at[:, 0, cell], diagonal, sems.at[cells]),
-        pltpu.make_async_copy(coupling, couple, sems.at[cells + 1]),
+        pltpu.make_async_copy(coupling, couple, arrivals.at[0]),
+        pltpu.make_async_copy(sigma.at[:, 0], source, arrivals.at[1]),
+        pltpu.make_async_copy(green.at[:, 0], columns, arrivals.at[2]),
     ]
     for shift in range(cells):
-        row = lax.rem(cell + shift, cells)
-        copies.append(pltpu.make_async_copy(screen.at[:, 0, row], blocks[shift], sems.at[shift]))
+        row = partner(cell, shift, cells)
+        copies.append(
+            pltpu.make_async_copy(screen.at[:, 0, row], blocks[shift], arrivals.at[3 + shift])
+        )
     for copy in copies:
         copy.start()
-    copies[0].wait()
-    diag_re = diagonal[0].astype(jnp.float32)
-    diag_im = diagonal[1].astype(jnp.float32)
+    for copy in copies[:3]:
+        copy.wait()
+    matrix = source_matrix(source[0], source[1])
+    leaving = []
+    for i in range(cells):
+        block = jnp.concatenate([columns[0, i], columns[1, i]], axis=1)
+        part = sandwich_block(block, matrix)
+        part = (part * couple[i, cell].astype(jnp.float32)).astype(jnp.bfloat16)
+        for owner in range(owners):
+            for c in range(2):
+                start = c * orbitals + owner * rows
+                placed[i, owner, c] = part[start : start + rows]
+        leaving.append(pltpu.make_async_copy(placed.at[i], chunks.at[:, i], departures.at[i]))
+        leaving[-1].start()
+    diag_re = columns[0, cell].astype(jnp.float32)
+    diag_im = columns[1, cell].astype(jnp.float32)
     difference = (diag_re - diag_re.T, diag_im + diag_im.T)
     for owner in range(owners):
         for c in range(2):
             here = difference[c][owner * rows : (owner + 1) * rows]
             spectral[owner ^ energy, c] = here.astype(jnp.bfloat16)
-    copies[1].wait()
     for shift in range(cells):
-        copies[2 + shift].wait()
-        weight = couple[lax.rem(cell + shift, cells), cell].astype(jnp.float32)
+        copies[3 + shift].wait()
+        weight = couple[partner(cell, shift, cells), cell].astype(jnp.float32)
         blocks[shift][...] = (blocks[shift][...].astype(jnp.float32) * weight).astype(jnp.bfloat16)
-
-
-def lesser_kernel(coupling, green, sigma, chunks):
-    cell = lax.axis_index("cell")
-    owners, cells, _, rows, _ = chunks.shape
-    orbitals = owners * rows
-    matrix = source_matrix(sigma[0, 0], sigma[1, 0])
-    for i in range(cells):
-        block = jnp.concatenate([green[0, 0, i], green[1, 0, i]], axis=1)
-        part = sandwich_block(block, matrix)
-        part = (part * coupling[i, cell].astype(jnp.float32)).astype(jnp.bfloat16)
-        for owner in range(owners):
-            for c in range(2):
-                start = c * orbitals + owner * rows
-                chunks[owner, i, c] = part[start : start + rows]
+    for copy in leaving:
+        copy.wait()
 
 
 def correlate_kernel(chunks, spectral, polar):
@@ -132,11 +142,10 @@
     owners, cells, _, height, width = rows.shape
     total = None
     for shift in range(cells):
-        j = lax.rem(cell + cells - shift, cells)
+        j = partner(cell, -shift, cells)
         parts = [rows[:, j, c].reshape(owners * height, width) for c in range(2)]
         if not shift:
-            polar[0] = parts[0]
-            polar[1] = parts[1]
+            polar[...] = jnp.stack(parts, axis=1)
         block = jnp.concatenate([blocks[shift][0], blocks[shift][1]], axis=1)
         part = sandwich_block(block, source_matrix(*parts))
         part = part.astype(jnp.bfloat16).astype(jnp.float32)
@@ -166,32 +175,30 @@
     rows = orbitals // owners
     half = functools.partial(jax.ShapeDtypeStruct, dtype=jnp.bfloat16)
     square = half((2, orbitals, orbitals))
-    spectral, own, *leaving = call(
-        prepare_kernel,
-        (half((owners, 2, rows, orbitals)),) + (square,) * cells,
-        (HBM, HBM, HBM),
-        pltpu.with_memory_space_constraint(coupling, HBM),
-        pltpu.with_memory_space_constraint(w_screened, HBM),
-        pltpu.with_memory_space_constraint(g_retarded, HBM),
+    chunks, spectral, own, *leaving = call(
+        lesser_kernel,
+        (half((owners, cells, 2, rows, orbitals)), half((owners, 2, rows, orbitals)))
+        + (square,) * cells,
+        (HBM,) * 4,
+        *(
+            pltpu.with_memory_space_constraint(array, HBM)
+            for array in (coupling, w_screened, g_retarded, sigma_lesser)
+        ),
         scratch=(
+            pltpu.SMEM(coupling.shape, coupling.dtype),
             pltpu.VMEM(square.shape, square.dtype),
-            pltpu.SMEM(coupling.shape, coupling.dtype),
-            pltpu.SemaphoreType.DMA((cells + 2,)),
+            pltpu.VMEM((2, cells, orbitals, orbitals), jnp.bfloat16),
+            pltpu.VMEM((cells, owners, 2, rows, orbitals), jnp.bfloat16),
+            pltpu.SemaphoreType.DMA((cells + 3,)),
+            pltpu.SemaphoreType.DMA((cells,)),
         ),
+        out_spaces=(HBM,) + (VMEM,) * (cells + 1),
     )
     arrived = []
     for shift, block in enumerate(leaving, 1):
-        pairs = [(k, (k + shift) % cells) for k in range(cells)]
+        pairs = [(k, partner(k, shift, cells)) for k in range(cells)]
         arrived.append(lax.ppermute(block, "cell", pairs))
     spectral = spread_spectral(spectral, owners)
-    chunks = call(
-        lesser_kernel,
-        half((owners, cells, 2, rows, orbitals)),
-        (SMEM, VMEM, VMEM),
-        coupling,
-        g_retarded,
-        sigma_lesser,
-    )
     chunks = lax.all_to_all(
         chunks.reshape(owners * cells, 2, rows, orbitals), ("energy", "cell"), 0, 0, tiled=True
     ).reshape(owners, cells, 2, rows, orbitals)
@@ -208,7 +215,7 @@
     anchor = polar[0, 0, 0] * 2
     polar, screened = call(
         screened_kernel,
-        (square, square),
+        (half((orbitals, 2, orbitals)), square),
         (HBM,) + (VMEM,) * (2 + len(arrived)),
         anchor,
         polar,
@@ -216,7 +223,7 @@
         *arrived,
     )
     return (
-        polar.reshape(1, 2, 1, orbitals * orbitals),
+        jnp.swapaxes(polar, 0, 1).reshape(1, 2, 1, orbitals * orbitals),
         screened.reshape(1, 2, 1, orbitals, orbitals),
     )
 

time: 42.9 us -> 41.5 us (0.967)
  starting transfers between devices: 18.5 us -> 17.3 us
  waiting for transfers between devices: 17.7 us -> 18.9 us
  local copies, waits for them, and re-layouts: 0.68 us -> 0.02 us
  Pallas kernels: 4.91 us -> 4.33 us
    ppermute x3, starting transfers between devices: 5.65 us -> 4.45 us  [on_device(): arrived.append(lax.ppermute(block, 'cell', pairs))]
    all_to_all x1, waiting for transfers between devices: 4.61 us -> 5.81 us  [on_device(): lax.all_to_all(polar.reshape(owners * cells, 2, rows, orbitals), ('energy...]
    reshape x1 -> x0, local copies, waits for them, and re-layouts: 0.65 us -> none  [on_device(): polar.reshape(1, 2, 1, orbitals * orbitals)]
    pallas_call x4 -> x3, Pallas kernels: 4.91 us -> 4.33 us  [call(): pl.pallas_call(body, out_shape=out_shape, in_specs=[pl.BlockSpec(memory_s...]
  transfers between devices with their start and end apart: 8 -> 8, of which waited for: 6 -> 5; matrix products, arithmetic and copies ran while one was open for 0% -> 0% of each run, Pallas kernels for 4% -> 0%
where the time goes in v3:
time: 41.5 us; the launch traced here: 41.3 us
  waiting for transfers between devices  18.9 us (46%)
  starting transfers between devices  17.3 us (42%)
  Pallas kernels  4.33 us (10%)
  between operations  0.71 us (2%)
    all_to_all x1, waiting for transfers between devices, on_device(): lax.all_to_all(chunks.reshape(owners * cells, 2, rows, orbitals), ('energ...  5.84 us
    all_to_all x1, waiting for transfers between devices, on_device(): lax.all_to_all(polar.reshape(owners * cells, 2, rows, orbitals), ('energy...  5.81 us
    ppermute x3, starting transfers between devices, spread_spectral(): got = lax.ppermute(sent, 'energy', [(k, k ^ bit) for k in range(owners)])  5.28 us
    all_to_all x1, starting transfers between devices, on_device(): lax.all_to_all(chunks.reshape(owners * cells, 2, rows, orbitals), ('energ...  4.92 us
    ppermute x3, starting transfers between devices, on_device(): arrived.append(lax.ppermute(block, 'cell', pairs))  4.45 us
    pallas_call x3, Pallas kernels, call(): pl.pallas_call(body, out_shape=out_shape, in_specs=[pl.BlockSpec(memory_s...  4.33 us
    ppermute x3, waiting for transfers between devices, on_device(): arrived.append(lax.ppermute(block, 'cell', pairs))  3.87 us
    ppermute x3, waiting for transfers between devices, spread_spectral(): got = lax.ppermute(sent, 'energy', [(k, k ^ bit) for k in range(owners)])  3.36 us
  transfers between devices with their start and end apart: 8, of which 5 were waited for; matrix products, arithmetic and copies ran while one was open for 0% of the time, Pallas kernels for 0%

profile of v3, /device:TPU:0, one launch (start us, length us, event | category | flops | bytes accessed | tf_op | source)
XLA Modules:
  0.0 41.3 jit_solution(9777866524182049390)
XLA Ops:
  0.6 2.2 %shard_map.59 = (bf16[8,4,2,16,128]{4,3,2,1,0:T(8,128)(2,1)}, bf16[8,2,16,128]{3,2,1,0:T(8,128)(2,1)S(1)}, bf16[2,128,128]{2,1,0:T(8,128)(2,1)S(1)}, bf16[2,128,...) custom-call(s32[4,4]{1,0:T(4,128)} %coupling.1, ...), custom_call_target="tpu_custom_call" | custom-call | tf_op jit(solution)/shard_map/pallas_call | solution.py:23
  2.9 0.6 %collective-permute-start = (bf16[4,2,16,128]{3,2,1,0:T(8,128)(2,1)S(1)}, bf16[4,2,16,128]{3,2,1,0:T(8,128)(2,1)S(1)}, u32[]{:S(2)}, u32[]{:S(2)}) collective-permute-start(bf16[4,2,16,128]{3,2,1,0:T(8,128)(2,1)S(1)} %pad_maximum_fusion.1), channel_id=1, source_target_pairs={{0,4},{4,0},{8,12},{12,8},{16,20},{20,16},{24,28},{28,24},{1,5},{5... | collective-permute-start | bytes 98312 | tf_op jit(solution)/shard_map/ppermute | solution.py:164
  3.5 0.9 %collective-permute-done = bf16[4,2,16,128]{3,2,1,0:T(8,128)(2,1)S(1)} collective-permute-done((bf16[4,2,16,128]{3,2,1,0:T(8,128)(2,1)S(1)}, bf16[4,2,16,128]{3,2,1,0:T(8,128)(2,1)S(1)}, u32[]{:S(2)}, u32[]{:S(2)}) %collective-permute-start) | collective-permute-done | bytes 32800 | tf_op jit(solution)/shard_map/ppermute | solution.py:164
  4.4 2.9 %collective-permute-start.1 = (bf16[4,2,16,128]{3,2,1,0:T(8,128)(2,1)S(1)}, bf16[4,2,16,128]{3,2,1,0:T(8,128)(2,1)S(1)}, u32[]{:S(2)}, u32[]{:S(2)}) collective-permute-start(bf16[4,2,16,128]{3,2,1,0:T(8,128)(2,1)S(1)} %pad_maximum_fusion.2), channel_id=1, source_target_pairs={{0,8},{4,12},{8,0},{12,4},{16,24},{20,28},{24,16},{28,20},{1,9},{5... | collective-permute-start | bytes 98312 | tf_op jit(solution)/shard_map/ppermute | solution.py:164
  7.2 4.9 %all-to-all-start = ((bf16[32,2,16,128]{3,2,1,0:T(8,128)(2,1)}), bf16[32,2,16,128]{3,2,1,0:T(8,128)(2,1)S(1)}, u32[]{:S(2)}, u32[]{:S(2)}) async-start(bf16[32,2,16,128]{3,2,1,0:T(8,128)(2,1)} %bitcast), calls=%async_computation | async-start | bytes 524288 | tf_op jit(solution)/shard_map/all_to_all | solution.py:202
  12.2 0.0 collective-permute-done.1
  12.2 1.8 %collective-permute-start.2 = (bf16[4,2,16,128]{3,2,1,0:T(8,128)(2,1)S(1)}, bf16[4,2,16,128]{3,2,1,0:T(8,128)(2,1)S(1)}, u32[]{:S(2)}, u32[]{:S(2)}) collective-permute-start(bf16[4,2,16,128]{3,2,1,0:T(8,128)(2,1)S(1)} %pad_maximum_fusion.3), channel_id=1, source_target_pairs={{0,16},{4,20},{8,24},{12,28},{16,0},{20,4},{24,8},{28,12},{1,17},{... | collective-permute-start | bytes 98312 | tf_op jit(solution)/shard_map/ppermute | solution.py:164
  14.0 2.5 %collective-permute-done.2 = bf16[4,2,16,128]{3,2,1,0:T(8,128)(2,1)S(1)} collective-permute-done((bf16[4,2,16,128]{3,2,1,0:T(8,128)(2,1)S(1)}, bf16[4,2,16,128]{3,2,1,0:T(8,128)(2,1)S(1)}, u32[]{:S(2)}, u32[]{:S(2)}) %collective-permute-start.2) | collective-permute-done | bytes 32800 | tf_op jit(solution)/shard_map/ppermute | solution.py:164
  16.6 5.8 %all-to-all-done = bf16[32,2,16,128]{3,2,1,0:T(8,128)(2,1)S(1)} async-done(((bf16[32,2,16,128]{3,2,1,0:T(8,128)(2,1)}), bf16[32,2,16,128]{3,2,1,0:T(8,128)(2,1)S(1)}, u32[]{:S(2)}, u32[]{:S(2)}) %all-to-all-start) | async-done | bytes 262176 | tf_op jit(solution)/shard_map/all_to_all | solution.py:202
  22.4 0.8 %shard_map.60 = bf16[8,4,2,16,128]{4,3,2,1,0:T(8,128)(2,1)} custom-call(bf16[8,4,2,16,128]{4,3,2,1,0:T(8,128)(2,1)S(1)} %bitcast.14, bf16[8,2,16,128]{3,2,1,0:T(8,128)(2,1)S(1)} %pad_maximum_fusion.spectral), custom_call_target="tpu_custom_call" | custom-call | tf_op jit(solution)/shard_map/pallas_call | solution.py:23
  23.2 2.7 %all-to-all-start.1 = ((bf16[32,2,16,128]{3,2,1,0:T(8,128)(2,1)}), bf16[32,2,16,128]{3,2,1,0:T(8,128)(2,1)S(1)}, u32[]{:S(2)}, u32[]{:S(2)}) async-start(bf16[32,2,16,128]{3,2,1,0:T(8,128)(2,1)} %bitcast.2), calls=%async_computation.1 | async-start | bytes 524288 | tf_op jit(solution)/shard_map/all_to_all | solution.py:212
  25.9 1.8 %collective-permute-start.3 = (bf16[2,128,128]{2,1,0:T(8,128)(2,1)S(1)}, bf16[2,128,128]{2,1,0:T(8,128)(2,1)S(1)}, u32[]{:S(2)}, u32[]{:S(2)}) collective-permute-start(bf16[2,128,128]{2,1,0:T(8,128)(2,1)S(1)} %get-tuple-element.13), channel_id=1, source_target_pairs={{0,1},{1,0},{2,3},{3,2},{4,5},{5,4},{6,7},{7,6},{8,9},{9,8},{10,11... | collective-permute-start | bytes 196616 | tf_op jit(solution)/shard_map/ppermute | solution.py:200
  27.7 2.4 %collective-permute-start.4 = (bf16[2,128,128]{2,1,0:T(8,128)(2,1)S(1)}, bf16[2,128,128]{2,1,0:T(8,128)(2,1)S(1)}, u32[]{:S(2)}, u32[]{:S(2)}) collective-permute-start(bf16[2,128,128]{2,1,0:T(8,128)(2,1)S(1)} %get-tuple-element.14), channel_id=1, source_target_pairs={{0,2},{1,3},{2,0},{3,1},{4,6},{5,7},{6,4},{7,5},{8,10},{9,11},{10,... | collective-permute-start | bytes 196616 | tf_op jit(solution)/shard_map/ppermute | solution.py:200
  30.2 0.2 collective-permute-start.5
  30.4 5.8 %all-to-all-done.1 = bf16[32,2,16,128]{3,2,1,0:T(8,128)(2,1)S(1)} async-done(((bf16[32,2,16,128]{3,2,1,0:T(8,128)(2,1)}), bf16[32,2,16,128]{3,2,1,0:T(8,128)(2,1)S(1)}, u32[]{:S(2)}, u32[]{:S(2)}) %all-to-all-start.1) | async-done | bytes 262176 | tf_op jit(solution)/shard_map/all_to_all | solution.py:212
  36.2 0.0 collective-permute-done.3.rest_1_
  36.2 3.9 %collective-permute-done.4.rest_2_ = bf16[2,128,128]{2,1,0:T(8,128)(2,1)S(1)} collective-permute-done((bf16[2,128,128]{2,1,0:T(8,128)(2,1)S(1)}, bf16[2,128,128]{2,1,0:T(8,128)(2,1)S(1)}, u32[]{:S(2)}, u32[]{:S(2)}) %collective-permute-start.4) | collective-permute-done | bytes 65568 | tf_op jit(solution)/shard_map/ppermute | solution.py:200
  40.0 0.0 collective-permute-done.5.rest_3_
  40.0 1.2 %shard_map.61 = (bf16[128,2,128]{2,1,0:T(2,128)(2,1)}, bf16[2,128,128]{2,1,0:T(8,128)(2,1)}) custom-call(bf16[16,128]{1,0:T(8,128)(2,1)S(1)} %fusion._, bf16[8,4,2,16,128]{4,3,2,1,0:T(8,128)(2,1)S(1)} %bitcast.13, bf16[2,128,128]{2,1,0:T(8,128)(2,1)S(1)} %get-tuple-element.12.rest_0_, bf16[2,128,128]{2,1,0:T(8,128)(2,1)S(1)} %collective-permute-done.3.rest_1_, ...), custom_call_target="tpu_custom_call" | custom-call | tf_op jit(solution)/shard_map/pallas_call | solution.py:23
  (8 shorter events, 0.1 us)
Async XLA Ops:
  2.9 1.4 %collective-permute-start = (bf16[4,2,16,128]{3,2,1,0:T(8,128)(2,1)S(1)}, bf16[4,2,16,128]{3,2,1,0:T(8,128)(2,1)S(1)}, u32[]{:S(2)}, u32[]{:S(2)}) collective-permute-start(bf16[4,2,16,128]{3,2,1,0:T(8,128)(2,1)S(1)} %pad_maximum_fusion.1), channel_id=1, source_target_pairs={{0,4},{4,0},{8,12},{12,8},{16,20},{20,16},{24,28},{28,24},{1,5},{5... | collective-permute-start | bytes 98312 | tf_op jit(solution)/shard_map/ppermute | solution.py:164
  4.4 7.8 %collective-permute-start.1 = (bf16[4,2,16,128]{3,2,1,0:T(8,128)(2,1)S(1)}, bf16[4,2,16,128]{3,2,1,0:T(8,128)(2,1)S(1)}, u32[]{:S(2)}, u32[]{:S(2)}) collective-permute-start(bf16[4,2,16,128]{3,2,1,0:T(8,128)(2,1)S(1)} %pad_maximum_fusion.2), channel_id=1, source_target_pairs={{0,8},{4,12},{8,0},{12,4},{16,24},{20,28},{24,16},{28,20},{1,9},{5... | collective-permute-start | bytes 98312 | tf_op jit(solution)/shard_map/ppermute | solution.py:164
  7.2 15.2 %all-to-all-start = ((bf16[32,2,16,128]{3,2,1,0:T(8,128)(2,1)}), bf16[32,2,16,128]{3,2,1,0:T(8,128)(2,1)S(1)}, u32[]{:S(2)}, u32[]{:S(2)}) async-start(bf16[32,2,16,128]{3,2,1,0:T(8,128)(2,1)} %bitcast), calls=%async_computation | async-start | bytes 524288 | tf_op jit(solution)/shard_map/all_to_all | solution.py:202
  12.2 4.3 %collective-permute-start.2 = (bf16[4,2,16,128]{3,2,1,0:T(8,128)(2,1)S(1)}, bf16[4,2,16,128]{3,2,1,0:T(8,128)(2,1)S(1)}, u32[]{:S(2)}, u32[]{:S(2)}) collective-permute-start(bf16[4,2,16,128]{3,2,1,0:T(8,128)(2,1)S(1)} %pad_maximum_fusion.3), channel_id=1, source_target_pairs={{0,16},{4,20},{8,24},{12,28},{16,0},{20,4},{24,8},{28,12},{1,17},{... | collective-permute-start | bytes 98312 | tf_op jit(solution)/shard_map/ppermute | solution.py:164
  23.2 12.9 %all-to-all-start.1 = ((bf16[32,2,16,128]{3,2,1,0:T(8,128)(2,1)}), bf16[32,2,16,128]{3,2,1,0:T(8,128)(2,1)S(1)}, u32[]{:S(2)}, u32[]{:S(2)}) async-start(bf16[32,2,16,128]{3,2,1,0:T(8,128)(2,1)} %bitcast.2), calls=%async_computation.1 | async-start | bytes 524288 | tf_op jit(solution)/shard_map/all_to_all | solution.py:212
  25.9 10.3 %collective-permute-start.3 = (bf16[2,128,128]{2,1,0:T(8,128)(2,1)S(1)}, bf16[2,128,128]{2,1,0:T(8,128)(2,1)S(1)}, u32[]{:S(2)}, u32[]{:S(2)}) collective-permute-start(bf16[2,128,128]{2,1,0:T(8,128)(2,1)S(1)} %get-tuple-element.13), channel_id=1, source_target_pairs={{0,1},{1,0},{2,3},{3,2},{4,5},{5,4},{6,7},{7,6},{8,9},{9,8},{10,11... | collective-permute-start | bytes 196616 | tf_op jit(solution)/shard_map/ppermute | solution.py:200
  27.7 12.3 %collective-permute-start.4 = (bf16[2,128,128]{2,1,0:T(8,128)(2,1)S(1)}, bf16[2,128,128]{2,1,0:T(8,128)(2,1)S(1)}, u32[]{:S(2)}, u32[]{:S(2)}) collective-permute-start(bf16[2,128,128]{2,1,0:T(8,128)(2,1)S(1)} %get-tuple-element.14), channel_id=1, source_target_pairs={{0,2},{1,3},{2,0},{3,1},{4,6},{5,7},{6,4},{7,5},{8,10},{9,11},{10,... | collective-permute-start | bytes 196616 | tf_op jit(solution)/shard_map/ppermute | solution.py:200
  30.2 9.9 %collective-permute-start.5 = (bf16[2,128,128]{2,1,0:T(8,128)(2,1)S(1)}, bf16[2,128,128]{2,1,0:T(8,128)(2,1)S(1)}, u32[]{:S(2)}, u32[]{:S(2)}) collective-permute-start(bf16[2,128,128]{2,1,0:T(8,128)(2,1)S(1)} %get-tuple-element.15), channel_id=1, source_target_pairs={{0,3},{1,2},{2,1},{3,0},{4,7},{5,6},{6,5},{7,4},{8,11},{9,10},{10,... | collective-permute-start | bytes 196616 | tf_op jit(solution)/shard_map/ppermute | solution.py:200

commit v4 on v3

--- a/solution.py
+++ b/solution.py
@@ -157,14 +157,16 @@
 
 def spread_spectral(spectral, owners):
     held = [spectral[distance] for distance in range(owners)]
-    bit = 1
-    while bit < owners:
-        moved = [distance for distance in range(owners) if distance & bit]
+
+    def exchange(moved, mask):
         sent = jnp.stack([held[distance] for distance in moved])
-        got = lax.ppermute(sent, "energy", [(k, k ^ bit) for k in range(owners)])
+        got = lax.ppermute(sent, "energy", [(k, k ^ mask) for k in range(owners)])
         for place, distance in enumerate(moved):
             held[distance] = got[place]
-        bit *= 2
+
+    exchange(range(1, owners, 2), 1)
+    for mask in range(2, owners, 2):
+        exchange((mask, mask + 1), mask)
     return jnp.stack(held)
 
 

time: 41.5 us -> 39.9 us (0.961)
  waiting for transfers between devices: 18.9 us -> 16.3 us
  starting transfers between devices: 17.3 us -> 18.2 us
    all_to_all x1, waiting for transfers between devices: 5.84 us -> 2.16 us  [on_device(): lax.all_to_all(chunks.reshape(owners * cells, 2, rows, orbitals), ('energ...]
    all_to_all x1, starting transfers between devices: 4.92 us -> 6.95 us  [on_device(): lax.all_to_all(chunks.reshape(owners * cells, 2, rows, orbitals), ('energ...]
    ppermute x3 -> x4, starting transfers between devices: 5.28 us -> 4.11 us  [exchange(): got = lax.ppermute(sent, 'energy', [(k, k ^ mask) for k in range(owners)])]
    ppermute x3 -> x4, waiting for transfers between devices: 3.36 us -> 4.44 us  [exchange(): got = lax.ppermute(sent, 'energy', [(k, k ^ mask) for k in range(owners)])]
  transfers between devices with their start and end apart: 8 -> 9, of which waited for: 5 -> 6; matrix products, arithmetic and copies ran while one was open for 0% -> 0% of each run, Pallas kernels for 0% -> 0%
where the time goes in v4:
time: 39.9 us; the launch traced here: 39.6 us
  starting transfers between devices  18.2 us (46%)
  waiting for transfers between devices  16.3 us (41%)
  Pallas kernels  4.33 us (11%)
  between operations  0.7 us (2%)
    all_to_all x1, starting transfers between devices, on_device(): lax.all_to_all(chunks.reshape(owners * cells, 2, rows, orbitals), ('energ...  6.95 us
    all_to_all x1, waiting for transfers between devices, on_device(): lax.all_to_all(polar.reshape(owners * cells, 2, rows, orbitals), ('energy...  5.81 us
    ppermute x3, starting transfers between devices, on_device(): arrived.append(lax.ppermute(block, 'cell', pairs))  4.45 us
    ppermute x4, waiting for transfers between devices, exchange(): got = lax.ppermute(sent, 'energy', [(k, k ^ mask) for k in range(owners)])  4.44 us
    pallas_call x3, Pallas kernels, call(): pl.pallas_call(body, out_shape=out_shape, in_specs=[pl.BlockSpec(memory_s...  4.33 us
    ppermute x4, starting transfers between devices, exchange(): got = lax.ppermute(sent, 'energy', [(k, k ^ mask) for k in range(owners)])  4.11 us
    ppermute x3, waiting for transfers between devices, on_device(): arrived.append(lax.ppermute(block, 'cell', pairs))  3.87 us
    all_to_all x1, starting transfers between devices, on_device(): lax.all_to_all(polar.reshape(owners * cells, 2, rows, orbitals), ('energy...  2.66 us
  transfers between devices with their start and end apart: 9, of which 6 were waited for; matrix products, arithmetic and copies ran while one was open for 0% of the time, Pallas kernels for 0%

profile of v4, /device:TPU:0, one launch (start us, length us, event | category | flops | bytes accessed | tf_op | source)
XLA Modules:
  0.0 39.6 jit_solution(16132102691959429347)
XLA Ops:
  0.6 2.2 %shard_map.59 = (bf16[8,4,2,16,128]{4,3,2,1,0:T(8,128)(2,1)}, bf16[8,2,16,128]{3,2,1,0:T(8,128)(2,1)S(1)}, bf16[2,128,128]{2,1,0:T(8,128)(2,1)S(1)}, bf16[2,128,...) custom-call(s32[4,4]{1,0:T(4,128)} %coupling.1, ...), custom_call_target="tpu_custom_call" | custom-call | tf_op jit(solution)/shard_map/pallas_call | solution.py:23
  2.9 0.6 %collective-permute-start = (bf16[4,2,16,128]{3,2,1,0:T(8,128)(2,1)S(1)}, bf16[4,2,16,128]{3,2,1,0:T(8,128)(2,1)S(1)}, u32[]{:S(2)}, u32[]{:S(2)}) collective-permute-start(bf16[4,2,16,128]{3,2,1,0:T(8,128)(2,1)S(1)} %pad_maximum_fusion), channel_id=1, source_target_pairs={{0,4},{4,0},{8,12},{12,8},{16,20},{20,16},{24,28},{28,24},{1,5},{5... | collective-permute-start | bytes 98312 | tf_op jit(solution)/shard_map/ppermute | solution.py:163
  3.5 6.9 %all-to-all-start = ((bf16[32,2,16,128]{3,2,1,0:T(8,128)(2,1)}), bf16[32,2,16,128]{3,2,1,0:T(8,128)(2,1)S(1)}, u32[]{:S(2)}, u32[]{:S(2)}) async-start(bf16[32,2,16,128]{3,2,1,0:T(8,128)(2,1)} %bitcast), calls=%async_computation | async-start | bytes 524288 | tf_op jit(solution)/shard_map/all_to_all | solution.py:204
  10.4 0.0 collective-permute-done
  10.5 1.8 %collective-permute-start.1 = (bf16[2,2,16,128]{3,2,1,0:T(8,128)(2,1)S(1)}, bf16[2,2,16,128]{3,2,1,0:T(8,128)(2,1)S(1)}, u32[]{:S(2)}, u32[]{:S(2)}) collective-permute-start(bf16[2,2,16,128]{3,2,1,0:T(8,128)(2,1)S(1)} %pad_maximum_fusion.1), channel_id=1, source_target_pairs={{0,8},{4,12},{8,0},{12,4},{16,24},{20,28},{24,16},{28,20},{1,9},{5... | collective-permute-start | bytes 49160 | tf_op jit(solution)/shard_map/ppermute | solution.py:163
  12.3 1.5 %collective-permute-start.2 = (bf16[2,2,16,128]{3,2,1,0:T(8,128)(2,1)S(1)}, bf16[2,2,16,128]{3,2,1,0:T(8,128)(2,1)S(1)}, u32[]{:S(2)}, u32[]{:S(2)}) collective-permute-start(bf16[2,2,16,128]{3,2,1,0:T(8,128)(2,1)S(1)} %pad_maximum_fusion.2), channel_id=1, source_target_pairs={{0,16},{4,20},{8,24},{12,28},{16,0},{20,4},{24,8},{28,12},{1,17},{... | collective-permute-start | bytes 49160 | tf_op jit(solution)/shard_map/ppermute | solution.py:163
  13.8 0.3 collective-permute-start.3
  14.0 0.5 %collective-permute-done.1 = bf16[2,2,16,128]{3,2,1,0:T(8,128)(2,1)S(1)} collective-permute-done((bf16[2,2,16,128]{3,2,1,0:T(8,128)(2,1)S(1)}, bf16[2,2,16,128]{3,2,1,0:T(8,128)(2,1)S(1)}, u32[]{:S(2)}, u32[]{:S(2)}) %collective-permute-start.1) | collective-permute-done | bytes 16416 | tf_op jit(solution)/shard_map/ppermute | solution.py:163
  14.5 1.6 %collective-permute-done.2 = bf16[2,2,16,128]{3,2,1,0:T(8,128)(2,1)S(1)} collective-permute-done((bf16[2,2,16,128]{3,2,1,0:T(8,128)(2,1)S(1)}, bf16[2,2,16,128]{3,2,1,0:T(8,128)(2,1)S(1)}, u32[]{:S(2)}, u32[]{:S(2)}) %collective-permute-start.2) | collective-permute-done | bytes 16416 | tf_op jit(solution)/shard_map/ppermute | solution.py:163
  16.2 2.3 %collective-permute-done.3 = bf16[2,2,16,128]{3,2,1,0:T(8,128)(2,1)S(1)} collective-permute-done((bf16[2,2,16,128]{3,2,1,0:T(8,128)(2,1)S(1)}, bf16[2,2,16,128]{3,2,1,0:T(8,128)(2,1)S(1)}, u32[]{:S(2)}, u32[]{:S(2)}) %collective-permute-start.3) | collective-permute-done | bytes 16416 | tf_op jit(solution)/shard_map/ppermute | solution.py:163
  18.5 2.2 %all-to-all-done = bf16[32,2,16,128]{3,2,1,0:T(8,128)(2,1)S(1)} async-done(((bf16[32,2,16,128]{3,2,1,0:T(8,128)(2,1)}), bf16[32,2,16,128]{3,2,1,0:T(8,128)(2,1)S(1)}, u32[]{:S(2)}, u32[]{:S(2)}) %all-to-all-start) | async-done | bytes 262176 | tf_op jit(solution)/shard_map/all_to_all | solution.py:204
  20.7 0.8 %shard_map.60 = bf16[8,4,2,16,128]{4,3,2,1,0:T(8,128)(2,1)} custom-call(bf16[8,4,2,16,128]{4,3,2,1,0:T(8,128)(2,1)S(1)} %bitcast.14, bf16[8,2,16,128]{3,2,1,0:T(8,128)(2,1)S(1)} %constant_dynamic-update-slice_fusion.spectral), custom_call_target="tpu_custom_call" | custom-call | tf_op jit(solution)/shard_map/pallas_call | solution.py:23
  21.5 2.7 %all-to-all-start.1 = ((bf16[32,2,16,128]{3,2,1,0:T(8,128)(2,1)}), bf16[32,2,16,128]{3,2,1,0:T(8,128)(2,1)S(1)}, u32[]{:S(2)}, u32[]{:S(2)}) async-start(bf16[32,2,16,128]{3,2,1,0:T(8,128)(2,1)} %bitcast.2), calls=%async_computation.1 | async-start | bytes 524288 | tf_op jit(solution)/shard_map/all_to_all | solution.py:214
  24.2 1.8 %collective-permute-start.4 = (bf16[2,128,128]{2,1,0:T(8,128)(2,1)S(1)}, bf16[2,128,128]{2,1,0:T(8,128)(2,1)S(1)}, u32[]{:S(2)}, u32[]{:S(2)}) collective-permute-start(bf16[2,128,128]{2,1,0:T(8,128)(2,1)S(1)} %get-tuple-element.13), channel_id=1, source_target_pairs={{0,1},{1,0},{2,3},{3,2},{4,5},{5,4},{6,7},{7,6},{8,9},{9,8},{10,11... | collective-permute-start | bytes 196616 | tf_op jit(solution)/shard_map/ppermute | solution.py:202
  26.0 2.4 %collective-permute-start.5 = (bf16[2,128,128]{2,1,0:T(8,128)(2,1)S(1)}, bf16[2,128,128]{2,1,0:T(8,128)(2,1)S(1)}, u32[]{:S(2)}, u32[]{:S(2)}) collective-permute-start(bf16[2,128,128]{2,1,0:T(8,128)(2,1)S(1)} %get-tuple-element.14), channel_id=1, source_target_pairs={{0,2},{1,3},{2,0},{3,1},{4,6},{5,7},{6,4},{7,5},{8,10},{9,11},{10,... | collective-permute-start | bytes 196616 | tf_op jit(solution)/shard_map/ppermute | solution.py:202
  28.4 0.2 collective-permute-start.6
  28.6 5.8 %all-to-all-done.1 = bf16[32,2,16,128]{3,2,1,0:T(8,128)(2,1)S(1)} async-done(((bf16[32,2,16,128]{3,2,1,0:T(8,128)(2,1)}), bf16[32,2,16,128]{3,2,1,0:T(8,128)(2,1)S(1)}, u32[]{:S(2)}, u32[]{:S(2)}) %all-to-all-start.1) | async-done | bytes 262176 | tf_op jit(solution)/shard_map/all_to_all | solution.py:214
  34.4 0.0 collective-permute-done.4.rest_1_
  34.4 3.9 %collective-permute-done.5.rest_2_ = bf16[2,128,128]{2,1,0:T(8,128)(2,1)S(1)} collective-permute-done((bf16[2,128,128]{2,1,0:T(8,128)(2,1)S(1)}, bf16[2,128,128]{2,1,0:T(8,128)(2,1)S(1)}, u32[]{:S(2)}, u32[]{:S(2)}) %collective-permute-start.5) | collective-permute-done | bytes 65568 | tf_op jit(solution)/shard_map/ppermute | solution.py:202
  38.3 0.0 collective-permute-done.6.rest_3_
  38.3 1.2 %shard_map.61 = (bf16[128,2,128]{2,1,0:T(2,128)(2,1)}, bf16[2,128,128]{2,1,0:T(8,128)(2,1)}) custom-call(bf16[16,128]{1,0:T(8,128)(2,1)S(1)} %fusion._, bf16[8,4,2,16,128]{4,3,2,1,0:T(8,128)(2,1)S(1)} %bitcast.13, bf16[2,128,128]{2,1,0:T(8,128)(2,1)S(1)} %get-tuple-element.12.rest_0_, bf16[2,128,128]{2,1,0:T(8,128)(2,1)S(1)} %collective-permute-done.4.rest_1_, ...), custom_call_target="tpu_custom_call" | custom-call | tf_op jit(solution)/shard_map/pallas_call | solution.py:23
  (10 shorter events, 0.1 us)
Async XLA Ops:
  2.9 7.5 %collective-permute-start = (bf16[4,2,16,128]{3,2,1,0:T(8,128)(2,1)S(1)}, bf16[4,2,16,128]{3,2,1,0:T(8,128)(2,1)S(1)}, u32[]{:S(2)}, u32[]{:S(2)}) collective-permute-start(bf16[4,2,16,128]{3,2,1,0:T(8,128)(2,1)S(1)} %pad_maximum_fusion), channel_id=1, source_target_pairs={{0,4},{4,0},{8,12},{12,8},{16,20},{20,16},{24,28},{28,24},{1,5},{5... | collective-permute-start | bytes 98312 | tf_op jit(solution)/shard_map/ppermute | solution.py:163
  3.5 17.2 %all-to-all-start = ((bf16[32,2,16,128]{3,2,1,0:T(8,128)(2,1)}), bf16[32,2,16,128]{3,2,1,0:T(8,128)(2,1)S(1)}, u32[]{:S(2)}, u32[]{:S(2)}) async-start(bf16[32,2,16,128]{3,2,1,0:T(8,128)(2,1)} %bitcast), calls=%async_computation | async-start | bytes 524288 | tf_op jit(solution)/shard_map/all_to_all | solution.py:204
  10.5 4.1 %collective-permute-start.1 = (bf16[2,2,16,128]{3,2,1,0:T(8,128)(2,1)S(1)}, bf16[2,2,16,128]{3,2,1,0:T(8,128)(2,1)S(1)}, u32[]{:S(2)}, u32[]{:S(2)}) collective-permute-start(bf16[2,2,16,128]{3,2,1,0:T(8,128)(2,1)S(1)} %pad_maximum_fusion.1), channel_id=1, source_target_pairs={{0,8},{4,12},{8,0},{12,4},{16,24},{20,28},{24,16},{28,20},{1,9},{5... | collective-permute-start | bytes 49160 | tf_op jit(solution)/shard_map/ppermute | solution.py:163
  12.3 3.8 %collective-permute-start.2 = (bf16[2,2,16,128]{3,2,1,0:T(8,128)(2,1)S(1)}, bf16[2,2,16,128]{3,2,1,0:T(8,128)(2,1)S(1)}, u32[]{:S(2)}, u32[]{:S(2)}) collective-permute-start(bf16[2,2,16,128]{3,2,1,0:T(8,128)(2,1)S(1)} %pad_maximum_fusion.2), channel_id=1, source_target_pairs={{0,16},{4,20},{8,24},{12,28},{16,0},{20,4},{24,8},{28,12},{1,17},{... | collective-permute-start | bytes 49160 | tf_op jit(solution)/shard_map/ppermute | solution.py:163
  13.8 4.7 %collective-permute-start.3 = (bf16[2,2,16,128]{3,2,1,0:T(8,128)(2,1)S(1)}, bf16[2,2,16,128]{3,2,1,0:T(8,128)(2,1)S(1)}, u32[]{:S(2)}, u32[]{:S(2)}) collective-permute-start(bf16[2,2,16,128]{3,2,1,0:T(8,128)(2,1)S(1)} %pad_maximum_fusion.3), channel_id=1, source_target_pairs={{0,24},{4,28},{8,16},{12,20},{16,8},{20,12},{24,0},{28,4},{1,25},{... | collective-permute-start | bytes 49160 | tf_op jit(solution)/shard_map/ppermute | solution.py:163
  21.5 12.9 %all-to-all-start.1 = ((bf16[32,2,16,128]{3,2,1,0:T(8,128)(2,1)}), bf16[32,2,16,128]{3,2,1,0:T(8,128)(2,1)S(1)}, u32[]{:S(2)}, u32[]{:S(2)}) async-start(bf16[32,2,16,128]{3,2,1,0:T(8,128)(2,1)} %bitcast.2), calls=%async_computation.1 | async-start | bytes 524288 | tf_op jit(solution)/shard_map/all_to_all | solution.py:214
  24.2 10.3 %collective-permute-start.4 = (bf16[2,128,128]{2,1,0:T(8,128)(2,1)S(1)}, bf16[2,128,128]{2,1,0:T(8,128)(2,1)S(1)}, u32[]{:S(2)}, u32[]{:S(2)}) collective-permute-start(bf16[2,128,128]{2,1,0:T(8,128)(2,1)S(1)} %get-tuple-element.13), channel_id=1, source_target_pairs={{0,1},{1,0},{2,3},{3,2},{4,5},{5,4},{6,7},{7,6},{8,9},{9,8},{10,11... | collective-permute-start | bytes 196616 | tf_op jit(solution)/shard_map/ppermute | solution.py:202
  26.0 12.3 %collective-permute-start.5 = (bf16[2,128,128]{2,1,0:T(8,128)(2,1)S(1)}, bf16[2,128,128]{2,1,0:T(8,128)(2,1)S(1)}, u32[]{:S(2)}, u32[]{:S(2)}) collective-permute-start(bf16[2,128,128]{2,1,0:T(8,128)(2,1)S(1)} %get-tuple-element.14), channel_id=1, source_target_pairs={{0,2},{1,3},{2,0},{3,1},{4,6},{5,7},{6,4},{7,5},{8,10},{9,11},{10,... | collective-permute-start | bytes 196616 | tf_op jit(solution)/shard_map/ppermute | solution.py:202
  28.4 9.9 %collective-permute-start.6 = (bf16[2,128,128]{2,1,0:T(8,128)(2,1)S(1)}, bf16[2,128,128]{2,1,0:T(8,128)(2,1)S(1)}, u32[]{:S(2)}, u32[]{:S(2)}) collective-permute-start(bf16[2,128,128]{2,1,0:T(8,128)(2,1)S(1)} %get-tuple-element.15), channel_id=1, source_target_pairs={{0,3},{1,2},{2,1},{3,0},{4,7},{5,6},{6,5},{7,4},{8,11},{9,10},{10,... | collective-permute-start | bytes 196616 | tf_op jit(solution)/shard_map/ppermute | solution.py:202

commit v5 on v4

--- a/solution.py
+++ b/solution.py
@@ -95,7 +95,7 @@
     for owner in range(owners):
         for c in range(2):
             here = difference[c][owner * rows : (owner + 1) * rows]
-            spectral[owner ^ energy, c] = here.astype(jnp.bfloat16)
+            spectral[owner ^ energy, c] = here
     for shift in range(cells):
         copies[3 + shift].wait()
         weight = couple[partner(cell, shift, cells), cell].astype(jnp.float32)
@@ -115,7 +115,7 @@
             total = chunks[e, 0, c].astype(jnp.float32)
             for j in range(1, cells):
                 total = total + chunks[e, j, c].astype(jnp.float32)
-            above = total + spectral[here ^ e, c].astype(jnp.float32)
+            above = total + spectral[here ^ e, c]
             low.append(total.astype(jnp.bfloat16).astype(jnp.float32))
             high.append(above.astype(jnp.bfloat16).astype(jnp.float32))
         lesser.append(low)
@@ -179,7 +179,10 @@
     square = half((2, orbitals, orbitals))
     chunks, spectral, own, *leaving = call(
         lesser_kernel,
-        (half((owners, cells, 2, rows, orbitals)), half((owners, 2, rows, orbitals)))
+        (
+            half((owners, cells, 2, rows, orbitals)),
+            jax.ShapeDtypeStruct((owners, 2, rows, orbitals), jnp.float32),
+        )
         + (square,) * cells,
         (HBM,) * 4,
         *(

time: 39.9 us -> 39.9 us (level)
  no operation moved by 1% of the time
where the time goes in v5:
time: 39.9 us; the launch traced here: 39.5 us
  starting transfers between devices  18.2 us (46%)
  waiting for transfers between devices  16.3 us (41%)
  Pallas kernels  4.33 us (11%)
  between operations  0.71 us (2%)
    all_to_all x1, starting transfers between devices, on_device(): lax.all_to_all(chunks.reshape(owners * cells, 2, rows, orbitals), ('energ...  6.95 us
    all_to_all x1, waiting for transfers between devices, on_device(): lax.all_to_all(polar.reshape(owners * cells, 2, rows, orbitals), ('energy...  5.81 us
    ppermute x4, waiting for transfers between devices, exchange(): got = lax.ppermute(sent, 'energy', [(k, k ^ mask) for k in range(owners)])  4.62 us
    ppermute x3, starting transfers between devices, on_device(): arrived.append(lax.ppermute(block, 'cell', pairs))  4.45 us
    pallas_call x3, Pallas kernels, call(): pl.pallas_call(body, out_shape=out_shape, in_specs=[pl.BlockSpec(memory_s...  4.33 us
    ppermute x4, starting transfers between devices, exchange(): got = lax.ppermute(sent, 'energy', [(k, k ^ mask) for k in range(owners)])  4.11 us
    ppermute x3, waiting for transfers between devices, on_device(): arrived.append(lax.ppermute(block, 'cell', pairs))  3.87 us
    all_to_all x1, starting transfers between devices, on_device(): lax.all_to_all(polar.reshape(owners * cells, 2, rows, orbitals), ('energy...  2.66 us
  transfers between devices with their start and end apart: 9, of which 6 were waited for; matrix products, arithmetic and copies ran while one was open for 0% of the time, Pallas kernels for 0%

profile of v5, /device:TPU:0, one launch (start us, length us, event | category | flops | bytes accessed | tf_op | source)
XLA Modules:
  0.0 39.5 jit_solution(9440758495964727564)
XLA Ops:
  0.6 2.2 %shard_map.59 = (bf16[8,4,2,16,128]{4,3,2,1,0:T(8,128)(2,1)}, f32[8,2,16,128]{3,2,1,0:T(8,128)S(1)}, bf16[2,128,128]{2,1,0:T(8,128)(2,1)S(1)}, bf16[2,128,128]{2...) custom-call(s32[4,4]{1,0:T(4,128)} %coupling.1, ...), custom_call_target="tpu_custom_call" | custom-call | tf_op jit(solution)/shard_map/pallas_call | solution.py:23
  2.9 0.6 %collective-permute-start = (f32[4,2,16,128]{3,2,1,0:T(8,128)S(1)}, f32[4,2,16,128]{3,2,1,0:T(8,128)S(1)}, u32[]{:S(2)}, u32[]{:S(2)}) collective-permute-start(f32[4,2,16,128]{3,2,1,0:T(8,128)S(1)} %pad_maximum_fusion), channel_id=1, source_target_pairs={{0,4},{4,0},{8,12},{12,8},{16,20},{20,16},{24,28},{28,24},{1,5},{5... | collective-permute-start | bytes 196616 | tf_op jit(solution)/shard_map/ppermute | solution.py:163
  3.5 6.9 %all-to-all-start = ((bf16[32,2,16,128]{3,2,1,0:T(8,128)(2,1)}), bf16[32,2,16,128]{3,2,1,0:T(8,128)(2,1)S(1)}, u32[]{:S(2)}, u32[]{:S(2)}) async-start(bf16[32,2,16,128]{3,2,1,0:T(8,128)(2,1)} %bitcast), calls=%async_computation | async-start | bytes 524288 | tf_op jit(solution)/shard_map/all_to_all | solution.py:207
  10.4 0.0 collective-permute-done
  10.5 1.8 %collective-permute-start.1 = (f32[2,2,16,128]{3,2,1,0:T(8,128)S(1)}, f32[2,2,16,128]{3,2,1,0:T(8,128)S(1)}, u32[]{:S(2)}, u32[]{:S(2)}) collective-permute-start(f32[2,2,16,128]{3,2,1,0:T(8,128)S(1)} %pad_maximum_fusion.1), channel_id=1, source_target_pairs={{0,8},{4,12},{8,0},{12,4},{16,24},{20,28},{24,16},{28,20},{1,9},{5... | collective-permute-start | bytes 98312 | tf_op jit(solution)/shard_map/ppermute | solution.py:163
  12.3 1.5 %collective-permute-start.2 = (f32[2,2,16,128]{3,2,1,0:T(8,128)S(1)}, f32[2,2,16,128]{3,2,1,0:T(8,128)S(1)}, u32[]{:S(2)}, u32[]{:S(2)}) collective-permute-start(f32[2,2,16,128]{3,2,1,0:T(8,128)S(1)} %pad_maximum_fusion.2), channel_id=1, source_target_pairs={{0,16},{4,20},{8,24},{12,28},{16,0},{20,4},{24,8},{28,12},{1,17},{... | collective-permute-start | bytes 98312 | tf_op jit(solution)/shard_map/ppermute | solution.py:163
  13.8 0.3 collective-permute-start.3
  14.0 1.3 %collective-permute-done.1 = f32[2,2,16,128]{3,2,1,0:T(8,128)S(1)} collective-permute-done((f32[2,2,16,128]{3,2,1,0:T(8,128)S(1)}, f32[2,2,16,128]{3,2,1,0:T(8,128)S(1)}, u32[]{:S(2)}, u32[]{:S(2)}) %collective-permute-start.1) | collective-permute-done | bytes 32800 | tf_op jit(solution)/shard_map/ppermute | solution.py:163
  15.4 1.1 %collective-permute-done.2 = f32[2,2,16,128]{3,2,1,0:T(8,128)S(1)} collective-permute-done((f32[2,2,16,128]{3,2,1,0:T(8,128)S(1)}, f32[2,2,16,128]{3,2,1,0:T(8,128)S(1)}, u32[]{:S(2)}, u32[]{:S(2)}) %collective-permute-start.2) | collective-permute-done | bytes 32800 | tf_op jit(solution)/shard_map/ppermute | solution.py:163
  16.4 2.2 %collective-permute-done.3 = f32[2,2,16,128]{3,2,1,0:T(8,128)S(1)} collective-permute-done((f32[2,2,16,128]{3,2,1,0:T(8,128)S(1)}, f32[2,2,16,128]{3,2,1,0:T(8,128)S(1)}, u32[]{:S(2)}, u32[]{:S(2)}) %collective-permute-start.3) | collective-permute-done | bytes 32800 | tf_op jit(solution)/shard_map/ppermute | solution.py:163
  18.7 2.0 %all-to-all-done = bf16[32,2,16,128]{3,2,1,0:T(8,128)(2,1)S(1)} async-done(((bf16[32,2,16,128]{3,2,1,0:T(8,128)(2,1)}), bf16[32,2,16,128]{3,2,1,0:T(8,128)(2,1)S(1)}, u32[]{:S(2)}, u32[]{:S(2)}) %all-to-all-start) | async-done | bytes 262176 | tf_op jit(solution)/shard_map/all_to_all | solution.py:207
  20.7 0.8 %shard_map.60 = bf16[8,4,2,16,128]{4,3,2,1,0:T(8,128)(2,1)} custom-call(bf16[8,4,2,16,128]{4,3,2,1,0:T(8,128)(2,1)S(1)} %bitcast.14, f32[8,2,16,128]{3,2,1,0:T(8,128)S(1)} %constant_dynamic-update-slice_fusion.spectral), custom_call_target="tpu_custom_call" | custom-call | tf_op jit(solution)/shard_map/pallas_call | solution.py:23
  21.5 2.7 %all-to-all-start.1 = ((bf16[32,2,16,128]{3,2,1,0:T(8,128)(2,1)}), bf16[32,2,16,128]{3,2,1,0:T(8,128)(2,1)S(1)}, u32[]{:S(2)}, u32[]{:S(2)}) async-start(bf16[32,2,16,128]{3,2,1,0:T(8,128)(2,1)} %bitcast.2), calls=%async_computation.1 | async-start | bytes 524288 | tf_op jit(solution)/shard_map/all_to_all | solution.py:217
  24.2 1.8 %collective-permute-start.4 = (bf16[2,128,128]{2,1,0:T(8,128)(2,1)S(1)}, bf16[2,128,128]{2,1,0:T(8,128)(2,1)S(1)}, u32[]{:S(2)}, u32[]{:S(2)}) collective-permute-start(bf16[2,128,128]{2,1,0:T(8,128)(2,1)S(1)} %get-tuple-element.13), channel_id=1, source_target_pairs={{0,1},{1,0},{2,3},{3,2},{4,5},{5,4},{6,7},{7,6},{8,9},{9,8},{10,11... | collective-permute-start | bytes 196616 | tf_op jit(solution)/shard_map/ppermute | solution.py:205
  26.0 2.4 %collective-permute-start.5 = (bf16[2,128,128]{2,1,0:T(8,128)(2,1)S(1)}, bf16[2,128,128]{2,1,0:T(8,128)(2,1)S(1)}, u32[]{:S(2)}, u32[]{:S(2)}) collective-permute-start(bf16[2,128,128]{2,1,0:T(8,128)(2,1)S(1)} %get-tuple-element.14), channel_id=1, source_target_pairs={{0,2},{1,3},{2,0},{3,1},{4,6},{5,7},{6,4},{7,5},{8,10},{9,11},{10,... | collective-permute-start | bytes 196616 | tf_op jit(solution)/shard_map/ppermute | solution.py:205
  28.4 0.2 collective-permute-start.6
  28.6 5.8 %all-to-all-done.1 = bf16[32,2,16,128]{3,2,1,0:T(8,128)(2,1)S(1)} async-done(((bf16[32,2,16,128]{3,2,1,0:T(8,128)(2,1)}), bf16[32,2,16,128]{3,2,1,0:T(8,128)(2,1)S(1)}, u32[]{:S(2)}, u32[]{:S(2)}) %all-to-all-start.1) | async-done | bytes 262176 | tf_op jit(solution)/shard_map/all_to_all | solution.py:217
  34.4 0.0 collective-permute-done.4.rest_1_
  34.4 3.9 %collective-permute-done.5.rest_2_ = bf16[2,128,128]{2,1,0:T(8,128)(2,1)S(1)} collective-permute-done((bf16[2,128,128]{2,1,0:T(8,128)(2,1)S(1)}, bf16[2,128,128]{2,1,0:T(8,128)(2,1)S(1)}, u32[]{:S(2)}, u32[]{:S(2)}) %collective-permute-start.5) | collective-permute-done | bytes 65568 | tf_op jit(solution)/shard_map/ppermute | solution.py:205
  38.3 0.0 collective-permute-done.6.rest_3_
  38.3 1.2 %shard_map.61 = (bf16[128,2,128]{2,1,0:T(2,128)(2,1)}, bf16[2,128,128]{2,1,0:T(8,128)(2,1)}) custom-call(bf16[16,128]{1,0:T(8,128)(2,1)S(1)} %fusion._, bf16[8,4,2,16,128]{4,3,2,1,0:T(8,128)(2,1)S(1)} %bitcast.13, bf16[2,128,128]{2,1,0:T(8,128)(2,1)S(1)} %get-tuple-element.12.rest_0_, bf16[2,128,128]{2,1,0:T(8,128)(2,1)S(1)} %collective-permute-done.4.rest_1_, ...), custom_call_target="tpu_custom_call" | custom-call | tf_op jit(solution)/shard_map/pallas_call | solution.py:23
  (10 shorter events, 0.1 us)
Async XLA Ops:
  2.9 7.5 %collective-permute-start = (f32[4,2,16,128]{3,2,1,0:T(8,128)S(1)}, f32[4,2,16,128]{3,2,1,0:T(8,128)S(1)}, u32[]{:S(2)}, u32[]{:S(2)}) collective-permute-start(f32[4,2,16,128]{3,2,1,0:T(8,128)S(1)} %pad_maximum_fusion), channel_id=1, source_target_pairs={{0,4},{4,0},{8,12},{12,8},{16,20},{20,16},{24,28},{28,24},{1,5},{5... | collective-permute-start | bytes 196616 | tf_op jit(solution)/shard_map/ppermute | solution.py:163
  3.5 17.2 %all-to-all-start = ((bf16[32,2,16,128]{3,2,1,0:T(8,128)(2,1)}), bf16[32,2,16,128]{3,2,1,0:T(8,128)(2,1)S(1)}, u32[]{:S(2)}, u32[]{:S(2)}) async-start(bf16[32,2,16,128]{3,2,1,0:T(8,128)(2,1)} %bitcast), calls=%async_computation | async-start | bytes 524288 | tf_op jit(solution)/shard_map/all_to_all | solution.py:207
  10.5 4.9 %collective-permute-start.1 = (f32[2,2,16,128]{3,2,1,0:T(8,128)S(1)}, f32[2,2,16,128]{3,2,1,0:T(8,128)S(1)}, u32[]{:S(2)}, u32[]{:S(2)}) collective-permute-start(f32[2,2,16,128]{3,2,1,0:T(8,128)S(1)} %pad_maximum_fusion.1), channel_id=1, source_target_pairs={{0,8},{4,12},{8,0},{12,4},{16,24},{20,28},{24,16},{28,20},{1,9},{5... | collective-permute-start | bytes 98312 | tf_op jit(solution)/shard_map/ppermute | solution.py:163
  12.3 4.1 %collective-permute-start.2 = (f32[2,2,16,128]{3,2,1,0:T(8,128)S(1)}, f32[2,2,16,128]{3,2,1,0:T(8,128)S(1)}, u32[]{:S(2)}, u32[]{:S(2)}) collective-permute-start(f32[2,2,16,128]{3,2,1,0:T(8,128)S(1)} %pad_maximum_fusion.2), channel_id=1, source_target_pairs={{0,16},{4,20},{8,24},{12,28},{16,0},{20,4},{24,8},{28,12},{1,17},{... | collective-permute-start | bytes 98312 | tf_op jit(solution)/shard_map/ppermute | solution.py:163
  13.8 4.9 %collective-permute-start.3 = (f32[2,2,16,128]{3,2,1,0:T(8,128)S(1)}, f32[2,2,16,128]{3,2,1,0:T(8,128)S(1)}, u32[]{:S(2)}, u32[]{:S(2)}) collective-permute-start(f32[2,2,16,128]{3,2,1,0:T(8,128)S(1)} %pad_maximum_fusion.3), channel_id=1, source_target_pairs={{0,24},{4,28},{8,16},{12,20},{16,8},{20,12},{24,0},{28,4},{1,25},{... | collective-permute-start | bytes 98312 | tf_op jit(solution)/shard_map/ppermute | solution.py:163
  21.5 12.9 %all-to-all-start.1 = ((bf16[32,2,16,128]{3,2,1,0:T(8,128)(2,1)}), bf16[32,2,16,128]{3,2,1,0:T(8,128)(2,1)S(1)}, u32[]{:S(2)}, u32[]{:S(2)}) async-start(bf16[32,2,16,128]{3,2,1,0:T(8,128)(2,1)} %bitcast.2), calls=%async_computation.1 | async-start | bytes 524288 | tf_op jit(solution)/shard_map/all_to_all | solution.py:217
  24.2 10.3 %collective-permute-start.4 = (bf16[2,128,128]{2,1,0:T(8,128)(2,1)S(1)}, bf16[2,128,128]{2,1,0:T(8,128)(2,1)S(1)}, u32[]{:S(2)}, u32[]{:S(2)}) collective-permute-start(bf16[2,128,128]{2,1,0:T(8,128)(2,1)S(1)} %get-tuple-element.13), channel_id=1, source_target_pairs={{0,1},{1,0},{2,3},{3,2},{4,5},{5,4},{6,7},{7,6},{8,9},{9,8},{10,11... | collective-permute-start | bytes 196616 | tf_op jit(solution)/shard_map/ppermute | solution.py:205
  26.0 12.3 %collective-permute-start.5 = (bf16[2,128,128]{2,1,0:T(8,128)(2,1)S(1)}, bf16[2,128,128]{2,1,0:T(8,128)(2,1)S(1)}, u32[]{:S(2)}, u32[]{:S(2)}) collective-permute-start(bf16[2,128,128]{2,1,0:T(8,128)(2,1)S(1)} %get-tuple-element.14), channel_id=1, source_target_pairs={{0,2},{1,3},{2,0},{3,1},{4,6},{5,7},{6,4},{7,5},{8,10},{9,11},{10,... | collective-permute-start | bytes 196616 | tf_op jit(solution)/shard_map/ppermute | solution.py:205
  28.4 9.9 %collective-permute-start.6 = (bf16[2,128,128]{2,1,0:T(8,128)(2,1)S(1)}, bf16[2,128,128]{2,1,0:T(8,128)(2,1)S(1)}, u32[]{:S(2)}, u32[]{:S(2)}) collective-permute-start(bf16[2,128,128]{2,1,0:T(8,128)(2,1)S(1)} %get-tuple-element.15), channel_id=1, source_target_pairs={{0,3},{1,2},{2,1},{3,0},{4,7},{5,6},{6,5},{7,4},{8,11},{9,10},{10,... | collective-permute-start | bytes 196616 | tf_op jit(solution)/shard_map/ppermute | solution.py:205
